TPU v7x, 256 devices: a whole 4x4x8 slice. The times are simulated.
256 devices in a mesh: grp: 4 (over x), dev: 64 (over z, y, core).
Axes of the slice: x: 4, y: 4, z: 8, core: 2. Of those that a mesh axis runs over, the one named last changes fastest.
Arguments:
- source_id: int32 [4194304], P(('grp', 'dev')), may hold values from 0 to 32767, as said below
- slot: int32 [4194304], P(('grp', 'dev')), may hold values from 0 to 127, as said below
- owner: int32 [32768], replicated, may hold values from 0 to 32767, as said below
- counts: int32 [32768], P(('grp', 'dev')), may hold values from 1 to 128, as said below
- partials: float32 [5, 4194304], P(None, ('grp', 'dev')), may hold values from -6 to 6
- residual: float32 [4194304], P(('grp', 'dev')), may hold values from -6 to 6
- weight: float32 [4194304], P(('grp', 'dev')), may hold values from 0.3 to 9
- prior: float32 [5, 32768], P(None, ('grp', 'dev')), may hold values from 0.5 to 4
Outputs:
- updates: float32 [5, 32768], P(None, ('grp', 'dev'))
- standardized: float32 [4194304], P(('grp', 'dev'))
- norm: float32 [], replicated
Inputs may be any that keep to these rules, and one draw needn't show every extreme that they name: A permutation: source s stands at owner position owner[s], and position p belongs to device p // 128. `source_id`: the rows of one device stand in 256 aligned blocks of 64 rows; block k holds only rows whose source's owner position lies in device k's range. Over all rows, each pair of a source and a slot below 128 appears exactly once. A row is an observation when its slot is below its source's count, else padding. Each device's block of counts holds 128 at least once.
All inputs are finite; a program needn't handle non-finite values.
Results may differ from a plain program's by a relative error of at most 0.0003.
Values sent between devices are 32-bit elements; how exact they have to be, the bound alone decides.
A program may use at most 64 MiB of HBM per device.

v0:
```python
import jax
import jax.numpy as jnp
from jax import lax
from jax.sharding import Mesh
from jax.sharding import PartitionSpec as P

DEV = ("dev_0", "dev_1", "dev_2")
DEV_GRP = ("dev_0", "dev_1", "dev_2", "grp")
GRP_DEV = ("grp", "dev_0", "dev_1", "dev_2")


def cut_along(value, dim, count):
    before, after = (value.shape[:dim], value.shape[dim + 1 :])
    return jnp.moveaxis(value.reshape(*before, count, -1, *after), dim, 0)


def joined_along(parts, dim):
    parts = jnp.moveaxis(parts, 0, dim)
    shape = parts.shape
    return parts.reshape(*shape[:dim], shape[dim] * shape[dim + 1], *shape[dim + 2 :])


def one_exchange(value, axis, axes, splits, concats):
    sizes = [lax.axis_size(a) for a in axes]
    parts = cut_along(value, splits[0], sizes[0])
    parts = jnp.moveaxis(cut_along(parts, splits[1] + 1, sizes[1]), 0, 1)
    inside = parts.shape[2:]
    parts = parts.reshape(-1, *inside)
    parts = lax.all_to_all(parts, axis, split_axis=0, concat_axis=0, tiled=True)
    parts = joined_along(parts.reshape(*sizes, *inside), concats[0] + 1)
    return joined_along(parts, concats[1])


def by_axis(value, axes):
    for axis in axes:
        value = lax.psum(value, axis)
    return value


def solve_blocks(normal, moments):
    params = len(moments)
    factor = {}
    for column in range(params):
        running = normal[column][column]
        for earlier in range(column):
            running = running - factor[column, earlier] ** 2
        pivot_value = jnp.sqrt(running)
        factor[column, column] = pivot_value
        for target in range(column + 1, params):
            current = normal[target][column]
            for earlier in range(column):
                current = current - factor[target, earlier] * factor[column, earlier]
            factor[target, column] = current / pivot_value
    forward = []
    for target in range(params):
        current = moments[target]
        for earlier in range(target):
            current = current - factor[target, earlier] * forward[earlier]
        forward.append(current / factor[target, target])
    backward = [None] * params
    for target in reversed(range(params)):
        current = forward[target]
        for later in range(target + 1, params):
            current = current - factor[later, target] * backward[later]
        backward[target] = current / factor[target, target]
    return jnp.stack(backward)


def spread_rows(table, onehot):
    return lax.dot_general(table, onehot, (((1,), (1,)), ((), ())), precision=lax.Precision.HIGHEST)


def body(source_id, slot, owner, counts, partials, residual, weight, prior):
    group_count = lax.axis_size("grp")
    member_count = lax.axis_size(DEV)
    params = partials.shape[0]
    fields_count = params + 2
    row_count = residual.shape[0]
    src_local = counts.shape[0]
    pad_slots = row_count // src_local
    block_rows = row_count // (group_count * member_count)
    position = owner[source_id]
    cell_index = position % src_local * pad_slots + slot
    fields = jnp.concatenate([partials, residual[None, :], weight[None, :]], axis=0)
    outgoing = (
        fields.reshape(fields_count, group_count, member_count, block_rows),
        cell_index.reshape(1, group_count, member_count, block_rows),
    )
    arrived, arrived_cell = (
        one_exchange(outgoing[0], DEV_GRP, (DEV, "grp"), (2, 1), (2, 1)),
        one_exchange(outgoing[1], DEV_GRP, (DEV, "grp"), (2, 1), (2, 1)),
    )
    arrived = arrived.reshape(fields_count, row_count)
    arrived_cell = arrived_cell.reshape(row_count)
    count_table = counts.astype(jnp.float32)[None, :]
    step_rows = min(row_count, 4096)
    step_count = row_count // step_rows
    columns = jnp.arange(src_local, dtype=jnp.int32)[None, :]
    pairs = [
        (first_idx, second_idx)
        for first_idx in range(params)
        for second_idx in range(first_idx, params)
    ]

    def block_view(index):
        start = index * step_rows
        piece = lax.dynamic_slice_in_dim(arrived, start, step_rows, 1)
        cells = lax.dynamic_slice_in_dim(arrived_cell, start, step_rows, 0)
        onehot = ((cells // pad_slots)[:, None] == columns).astype(jnp.float32)
        row_counts = spread_rows(count_table, onehot)[0]
        live = ((cells % pad_slots).astype(jnp.float32) < row_counts).astype(jnp.float32)
        return (piece, onehot, live)

    def accumulate(index, total):
        piece, onehot, live = block_view(index)
        slopes = piece[0:params]
        observed = piece[params]
        weighted = slopes * (piece[params + 1] * live)[None]
        terms = [weighted[first_idx] * slopes[second_idx] for first_idx, second_idx in pairs]
        terms = terms + [weighted[first_idx] * observed for first_idx in range(params)]
        stats = jnp.stack(terms)
        return total + jnp.dot(stats, onehot, precision=lax.Precision.HIGHEST)

    sums = lax.fori_loop(
        0, step_count, accumulate, jnp.zeros((len(pairs) + params, src_local), jnp.float32)
    )
    normal = [[None] * params for _ in range(params)]
    for pair_idx, (first_idx, second_idx) in enumerate(pairs):
        entry = sums[pair_idx]
        if first_idx == second_idx:
            entry = entry + prior[first_idx]
        normal[first_idx][second_idx] = entry
        normal[second_idx][first_idx] = entry
    moments = [sums[len(pairs) + first_idx] for first_idx in range(params)]
    updates = solve_blocks(normal, moments)

    def refit(index, fresh_rows):
        piece, onehot, live = block_view(index)
        fitted = jnp.sum(piece[0:params] * spread_rows(updates, onehot), axis=0)
        fresh_block = (piece[params] - fitted) * live
        return lax.dynamic_update_slice_in_dim(fresh_rows, fresh_block, index * step_rows, 0)

    fresh_cells = lax.fori_loop(0, step_count, refit, jnp.zeros((row_count,), jnp.float32))
    returned = one_exchange(
        fresh_cells.reshape(1, group_count, member_count, block_rows),
        GRP_DEV,
        ("grp", DEV),
        (1, 2),
        (1, 2),
    )
    fresh = returned.reshape(row_count)
    totals = by_axis(
        jnp.stack([jnp.sum(weight * fresh * fresh), jnp.sum(counts.astype(jnp.float32))]), GRP_DEV
    )
    norm = jnp.sqrt(totals[0] / totals[1] + 1e-06)
    return (updates, fresh * jnp.sqrt(weight) / norm, norm)


def solution(mesh):
    split = Mesh(
        mesh.devices.reshape(mesh.shape["grp"], 8, 4, 2), ("grp", "dev_0", "dev_1", "dev_2")
    )
    in_specs = (
        P(GRP_DEV),
        P(GRP_DEV),
        P(),
        P(GRP_DEV),
        P(None, GRP_DEV),
        P(GRP_DEV),
        P(GRP_DEV),
        P(None, GRP_DEV),
    )
    out_specs = (P(None, GRP_DEV), P(GRP_DEV), P())
    return jax.shard_map(body, mesh=split, in_specs=in_specs, out_specs=out_specs, check_vma=False)
```

profile of v0, /device:TPU:1, one launch (start us, length us, event | category | flops | bytes accessed | tf_op | source)
XLA Modules:
  0.0 240.2 jit_solution(943188109928438827)
XLA Ops:
  1.6 90.5 %gather_fusion = s32[16384]{0:T(1024)S(1)} fusion(s32[32768]{0:T(1024)S(1)} %copy-done, s32[16384]{0:T(1024)S(1)} %fusion.29), kind=kCustom, calls=%fused_computation | custom fusion | bytes 196608 | tf_op jit(solution)/shard_map/gather | solution.py:82
  93.0 15.6 %all-to-all-start.1 = ((s32[256,1,1,1,64]{4,3,2,1,0:T(1,128)}), s32[256,1,1,1,64]{4,3,2,1,0:T(1,128)S(1)}, u32[]{:S(2)}, u32[]{:S(2)}) async-start(s32[256,1,1,1,64]{4,3,2,1,0:T(1,128)} %bitcast.10), calls=%async_computation.1 | async-start | bytes 262144 | tf_op jit(solution)/shard_map/all_to_all | solution.py:29
  112.1 1.6 reshape.81
  113.7 7.8 %all-to-all-done.1 = s32[256,1,1,1,64]{4,3,2,1,0:T(1,128)S(1)} async-done(((s32[256,1,1,1,64]{4,3,2,1,0:T(1,128)}), s32[256,1,1,1,64]{4,3,2,1,0:T(1,128)S(1)}, u32[]{:S(2)}, u32[]{:S(2)}) %all-to-all-start.1) | async-done | bytes 65568 | tf_op jit(solution)/shard_map/all_to_all | solution.py:29
  121.4 6.0 %all-to-all-start = ((f32[256,1,448]{2,1,0:T(1,128)}), f32[256,1,448]{2,1,0:T(1,128)S(1)}, u32[]{:S(2)}, u32[]{:S(2)}) async-start(f32[256,1,448]{2,1,0:T(1,128)} %reshape.81), calls=%async_computation | async-start | bytes 1048576 | tf_op jit(solution)/shard_map/all_to_all | solution.py:29
  127.5 19.7 %all-to-all-done = f32[256,1,448]{2,1,0:T(1,128)S(1)} async-done(((f32[256,1,448]{2,1,0:T(1,128)}), f32[256,1,448]{2,1,0:T(1,128)S(1)}, u32[]{:S(2)}, u32[]{:S(2)}) %all-to-all-start) | async-done | bytes 458784 | tf_op jit(solution)/shard_map/all_to_all | solution.py:29
  147.2 1.9 reduce.1
  150.6 14.9 %while.33 = (s32[]{:T(128)}, f32[20,128]{1,0:T(8,128)S(1)}, f32[7,16384]{1,0:T(8,128)S(1)}, s32[16384]{0:T(1024)S(1)}, f32[1,128]{1,0:T(1,128)S(1)}, /*index=5*/...) while((s32[]{:T(128)}, f32[20,128]{1,0:T(8,128)S(1)}, ...), condition=%wide.region_1.2_spmd.clone, body=%wide.region_0.1_spmd.clone.sunk | while | flops 133391376 | bytes 2028365 | solution.py:124
  150.7 1.5 fusion.48
  153.3 1.0 fusion.50
  154.4 1.5 fusion.48
  157.0 1.0 fusion.50
  158.1 1.5 fusion.48
  160.8 1.0 fusion.50
  161.8 1.5 fusion.48
  164.5 1.0 fusion.50
  165.7 12.7 %while.32 = (s32[]{:T(128)}, f32[16384]{0:T(1024)S(1)}, s32[16384]{0:T(1024)S(1)}, f32[1,128]{1,0:T(1,128)S(1)}, f32[7,16384]{1,0:T(8,128)S(1)}, /*index=5*/f32[...) while((s32[]{:T(128)}, f32[16384]{0:T(1024)S(1)}, ...), condition=%wide.region_4.5_spmd.clone, body=%wide.region_2.4_spmd.clone.sunk | while | flops 38952968 | bytes 306359 | solution.py:143
  165.8 1.5 fusion.44
  167.3 1.5 fusion.45
  168.9 1.5 fusion.44
  170.5 1.5 fusion.45
  172.1 1.5 fusion.44
  173.6 1.5 fusion.45
  175.3 1.5 fusion.44
  176.8 1.5 fusion.45
  179.2 6.5 %all-to-all-start.2 = ((f32[256,1,1,1,64]{4,3,2,1,0:T(1,128)}), f32[256,1,1,1,64]{4,3,2,1,0:T(1,128)S(1)}, u32[]{:S(2)}, u32[]{:S(2)}) async-start(f32[256,1,1,1,64]{4,3,2,1,0:T(1,128)} %bitcast.14), calls=%async_computation.2 | async-start | bytes 262144 | tf_op jit(solution)/shard_map/all_to_all | solution.py:29
  186.2 12.2 %all-to-all-done.2 = f32[256,1,1,1,64]{4,3,2,1,0:T(1,128)S(1)} async-done(((f32[256,1,1,1,64]{4,3,2,1,0:T(1,128)}), f32[256,1,1,1,64]{4,3,2,1,0:T(1,128)S(1)}, u32[]{:S(2)}, u32[]{:S(2)}) %all-to-all-start.2) | async-done | bytes 65568 | tf_op jit(solution)/shard_map/all_to_all | solution.py:29
  199.2 1.4 pad_maximum_fusion.1
  200.6 6.8 %psum.28 = f32[2]{0:T(128)S(1)} all-reduce(f32[2]{0:T(128)S(1)} %pad_maximum_fusion.1), channel_id=1, replica_groups=mesh['grp'=4,'dev_0'=8,'dev_1'=4,'dev_2'=2] {'grp'}, use_global_device_ids=true, to_apply=%region_7.8 | all-reduce | flops 2 | bytes 16 | tf_op jit(solution)/shard_map/psum | solution.py:36
  207.4 11.5 %psum.29 = f32[2]{0:T(128)S(1)} all-reduce(f32[2]{0:T(128)S(1)} %psum.28), channel_id=1, replica_groups=mesh['grp'=4,'dev_0'=8,'dev_1'=4,'dev_2'=2] {'dev_0'}, use_global_device_ids=true, to_apply=%region_8.9 | all-reduce | flops 2 | bytes 16 | tf_op jit(solution)/shard_map/psum | solution.py:36
  218.9 6.6 %psum.30 = f32[2]{0:T(128)S(1)} all-reduce(f32[2]{0:T(128)S(1)} %psum.29), channel_id=1, replica_groups=mesh['grp'=4,'dev_0'=8,'dev_1'=4,'dev_2'=2] {'dev_1'}, use_global_device_ids=true, to_apply=%region_9.10 | all-reduce | flops 2 | bytes 16 | tf_op jit(solution)/shard_map/psum | solution.py:36
  225.5 10.9 %psum.31 = f32[2]{0:T(128)S(1)} all-reduce(f32[2]{0:T(128)S(1)} %psum.30), channel_id=1, replica_groups=mesh['grp'=4,'dev_0'=8,'dev_1'=4,'dev_2'=2] {'dev_2'}, use_global_device_ids=true, to_apply=%region_10.11 | all-reduce | flops 2 | bytes 16 | tf_op jit(solution)/shard_map/psum | solution.py:36
  (89 shorter events, 15.5 us)
Async XLA Ops:
  0.6 0.9 copy-start
  1.6 90.5 %copy-start.3 = (s32[16384]{0:T(1024)S(1)}, s32[16384]{0:T(1024)}, u32[]{:S(2)}) copy-start(s32[16384]{0:T(1024)} %param.13) | copy-start | bytes 196612
  92.1 16.5 %copy-start.2 = (f32[5,16384]{1,0:T(8,128)S(1)}, f32[5,16384]{1,0:T(8,128)}, u32[]{:S(2)}) copy-start(f32[5,16384]{1,0:T(8,128)} %param.16) | copy-start | bytes 983044
  93.0 28.4 %all-to-all-start.1 = ((s32[256,1,1,1,64]{4,3,2,1,0:T(1,128)}), s32[256,1,1,1,64]{4,3,2,1,0:T(1,128)S(1)}, u32[]{:S(2)}, u32[]{:S(2)}) async-start(s32[256,1,1,1,64]{4,3,2,1,0:T(1,128)} %bitcast.10), calls=%async_computation.1 | async-start | bytes 262144 | tf_op jit(solution)/shard_map/all_to_all | solution.py:29
  108.7 0.8 copy-start.4
  108.9 0.8 copy-start.1
  112.1 15.3 %copy-start.7 = (s32[128]{0:T(128)S(1)}, s32[128]{0:T(128)}, u32[]{:S(2)}) copy-start(s32[128]{0:T(128)} %param.15) | copy-start | bytes 1540
  121.4 25.8 %all-to-all-start = ((f32[256,1,448]{2,1,0:T(1,128)}), f32[256,1,448]{2,1,0:T(1,128)S(1)}, u32[]{:S(2)}, u32[]{:S(2)}) async-start(f32[256,1,448]{2,1,0:T(1,128)} %reshape.81), calls=%async_computation | async-start | bytes 1048576 | tf_op jit(solution)/shard_map/all_to_all | solution.py:29
  150.6 14.9 %copy-start.6 = (f32[5,128]{1,0:T(8,128)S(1)}, f32[5,128]{1,0:T(8,128)}, u32[]{:S(2)}) copy-start(f32[5,128]{1,0:T(8,128)} %param.19) | copy-start | bytes 7684
  178.4 60.6 %copy-start.5 = (f32[5,128]{1,0:T(8,128)}, f32[5,128]{1,0:T(8,128)S(1)}, u32[]{:S(2)}) copy-start(f32[5,128]{1,0:T(8,128)S(1)} %get-tuple-element.645) | copy-start | bytes 7684
  179.2 19.3 %all-to-all-start.2 = ((f32[256,1,1,1,64]{4,3,2,1,0:T(1,128)}), f32[256,1,1,1,64]{4,3,2,1,0:T(1,128)S(1)}, u32[]{:S(2)}, u32[]{:S(2)}) async-start(f32[256,1,1,1,64]{4,3,2,1,0:T(1,128)} %bitcast.14), calls=%async_computation.2 | async-start | bytes 262144 | tf_op jit(solution)/shard_map/all_to_all | solution.py:29
where the time goes:
time: 241 us; the launch traced here: 240 us
  local copies, waits for them, and re-layouts  101 us (42%)
  waiting for transfers between devices  39.7 us (16%)
  blocking collectives  35.9 us (15%)
  starting transfers between devices  28.1 us (12%)
  matrix products  21.7 us (9%)
  other arithmetic  9.7 us (4%)
  between operations  3.45 us (1%)
    gather x1, local copies, waits for them, and re-layouts, body(): position = owner[source_id]  90.5 us
    all_to_all x3, waiting for transfers between devices, one_exchange(): parts = lax.all_to_all(parts, axis, split_axis=0, concat_axis=0, tiled=True)  39.7 us
    psum x4, blocking collectives, by_axis(): value = lax.psum(value, axis)  35.9 us
    all_to_all x3, starting transfers between devices, one_exchange(): parts = lax.all_to_all(parts, axis, split_axis=0, concat_axis=0, tiled=True)  28.1 us
    dot_general x12, matrix products, spread_rows(): lax.dot_general(table, onehot, (((1,), (1,)), ((), ())), precision=lax.Pr...  17.7 us
  transfers between devices with their start and end apart: 3, of which 3 were waited for; matrix products, arithmetic and copies ran while one was open for 2% of the time, Pallas kernels for 0%

commit v1 on v0

v1 whole, which is shorter than its diff:
```python
import functools

import jax
import jax.numpy as jnp
from jax import lax
from jax.experimental import pallas as pl
from jax.experimental.pallas import tpu as pltpu
from jax.sharding import PartitionSpec as P

MESH = pl.DeviceIdType.MESH
F32 = jnp.float32
BF16 = jnp.bfloat16
LANES = 128
ROWS_Y = 4
CORES = 2
PARAMS = 5
GROUP = 16


def split_bf16(value):
    high = value.astype(BF16).astype(F32)
    rest = value - high
    middle = rest.astype(BF16).astype(F32)
    return high, middle, rest - middle


def column_of(row):
    square = (LANES, LANES)
    diagonal = lax.broadcasted_iota(jnp.int32, square, 0) == lax.broadcasted_iota(jnp.int32, square, 1)
    return jnp.sum(jnp.where(diagonal, jnp.broadcast_to(row, square), 0.0), axis=1, keepdims=True)


def solve_blocks(normal, moments):
    params = len(moments)
    factor = {}
    for column in range(params):
        running = normal[column][column]
        for earlier in range(column):
            running = running - factor[column, earlier] ** 2
        pivot_value = jnp.sqrt(running)
        factor[column, column] = pivot_value
        for target in range(column + 1, params):
            current = normal[target][column]
            for earlier in range(column):
                current = current - factor[target, earlier] * factor[column, earlier]
            factor[target, column] = current / pivot_value
    forward = []
    for target in range(params):
        current = moments[target]
        for earlier in range(target):
            current = current - factor[target, earlier] * forward[earlier]
        forward.append(current / factor[target, target])
    backward = [None] * params
    for target in reversed(range(params)):
        current = forward[target]
        for later in range(target + 1, params):
            current = current - factor[later, target] * backward[later]
        backward[target] = current / factor[target, target]
    return backward


def kernel(
    shape,
    source_ref,
    slot_ref,
    owner_ref,
    counts_ref,
    partials_ref,
    residual_ref,
    weight_ref,
    prior_ref,
    updates_ref,
    standard_ref,
    norm_ref,
    send_buf,
    recv_buf,
    halves,
    onehot,
    stats,
    total,
    table,
    facts,
    sums,
    other_sums,
    update_rows,
    fresh_out,
    fresh_in,
    square_out,
    square_in,
    square_total,
    send_sem,
    recv_sem,
    pair_send,
    pair_recv,
    back_send,
    back_recv,
):
    size_x, size_y, size_z = shape
    chips = size_x * size_y * size_z
    groups = chips // GROUP
    me_x = lax.axis_index("grp")
    me_dev = lax.axis_index("dev")
    core = me_dev % CORES
    me_y = (me_dev // CORES) % size_y
    me_z = me_dev // (CORES * size_y)
    me_chip = (me_x * size_z + me_z) * size_y + me_y

    def offset(p):
        q = p // GROUP
        inside = GROUP - 1 - p % GROUP
        dz = (size_z // 2 + ((q + 1) // 2) * (1 - 2 * (q % 2))) % size_z
        return inside // size_y, inside % size_y, dz

    def place(x, y, z):
        return (x, (z * size_y + y) * CORES + core), (x * size_z + z) * size_y + y

    def ahead(p):
        dx, dy, dz = offset(p)
        return place((me_x + dx) % size_x, (me_y + dy) % size_y, (me_z + dz) % size_z)

    def behind(p):
        dx, dy, dz = offset(p)
        return place(
            (me_x + size_x - dx) % size_x,
            (me_y + size_y - dy) % size_y,
            (me_z + size_z - dz) % size_z,
        )

    partner = (me_x, me_dev + 1 - 2 * core)
    barrier = pltpu.get_barrier_semaphore()

    def greet(p, carry):
        device, _ = ahead(p)
        pl.semaphore_signal(barrier, inc=1, device_id=device, device_id_type=MESH)
        return carry

    pl.semaphore_signal(barrier, inc=1, device_id=partner, device_id_type=MESH)
    lax.fori_loop(0, chips - 1, greet, 0)

    for block in range(chips // 8):
        rows = pl.ds(block * 8, 8)
        cell = (source_ref[rows, :] * LANES + slot_ref[rows, :]).astype(F32)
        send_buf[pl.ds(block * 64 + PARAMS, 8, stride=8), :] = residual_ref[rows, :]
        send_buf[pl.ds(block * 64 + PARAMS + 1, 8, stride=8), :] = weight_ref[rows, :]
        send_buf[pl.ds(block * 64 + PARAMS + 2, 8, stride=8), :] = cell
        for tile in range(block * 8, block * 8 + 8):
            send_buf[tile * 8 : tile * 8 + PARAMS, :] = partials_ref[:, tile * LANES : (tile + 1) * LANES]
    facts[pl.ds(pl.multiple_of(core * 8, 8), 8), :] = jnp.concatenate(
        [prior_ref[...], counts_ref[...].astype(F32), jnp.zeros((2, LANES), F32)], axis=0
    )

    sublane = lax.broadcasted_iota(jnp.int32, (LANES, LANES), 0)
    lane = lax.broadcasted_iota(jnp.int32, (1, LANES), 1)
    for side in range(CORES):
        base = (me_chip * CORES + side) * LANES

        def look(step, found):
            rows = owner_ref[pl.ds(pl.multiple_of(step * 8, 8), 8), :] - base
            for row in range(8):
                here = lane + (step * 8 + row) * LANES
                found = jnp.where(rows[row : row + 1, :] == sublane, here, found)
            return found

        found = lax.fori_loop(0, owner_ref.shape[0] // 8, look, jnp.zeros((LANES, LANES), jnp.int32))
        first = jnp.sum(found.astype(F32), axis=1, keepdims=True) * LANES
        table[side, 0] = jnp.broadcast_to(first, (LANES, LANES))

    pl.semaphore_wait(barrier, chips)

    facts_copy = pltpu.make_async_remote_copy(
        src_ref=facts.at[pl.ds(pl.multiple_of(core * 8, 8), 8), :],
        dst_ref=facts.at[pl.ds(pl.multiple_of(core * 8, 8), 8), :],
        send_sem=pair_send.at[0],
        recv_sem=pair_recv.at[0],
        device_id=partner,
        device_id_type=MESH,
    )
    facts_copy.start()

    def tile_copy(p):
        device, chip = ahead(p)
        return pltpu.make_async_remote_copy(
            src_ref=send_buf.at[pl.ds(pl.multiple_of(chip * 8, 8), 8), :],
            dst_ref=recv_buf.at[pl.ds(pl.multiple_of(p * 8, 8), 8), :],
            send_sem=send_sem,
            recv_sem=recv_sem.at[p // GROUP],
            device_id=device,
            device_id_type=MESH,
        )

    def send_tile(p, carry):
        tile_copy(p).start()
        return carry

    lax.fori_loop(0, chips - 1, send_tile, 0)
    recv_buf[(chips - 1) * 8 : chips * 8, :] = send_buf[pl.ds(pl.multiple_of(me_chip * 8, 8), 8), :]

    facts_copy.wait()
    for side in range(CORES):
        count = column_of(facts[side * 8 + PARAMS : side * 8 + PARAMS + 1, :])
        table[side, 0] = table[side, 0] + (count - 1.0) * 0.5
        table[side, 1] = jnp.broadcast_to(count * 0.5, (LANES, LANES))

    def wait_rows(source, target, count, send, recv, to):
        return pltpu.make_async_remote_copy(
            src_ref=source.at[pl.ds(0, count)],
            dst_ref=target.at[pl.ds(0, count)],
            send_sem=send,
            recv_sem=recv,
            device_id=to,
            device_id_type=MESH,
        )

    low = lax.broadcasted_iota(jnp.int32, (8, LANES), 1) < LANES // 2
    total[...] = jnp.zeros_like(total)

    def gather_group(q):
        def pair(v, carry):
            start = pl.multiple_of(q * GROUP * 8 + v * 16, 16)
            even = recv_buf[pl.ds(start, 8), :]
            odd = recv_buf[pl.ds(start + 8, 8), :]
            left = jnp.where(low, even, pltpu.roll(odd, LANES // 2, 1))
            right = jnp.where(low, pltpu.roll(even, LANES // 2, 1), odd)
            for side, rows in ((0, left), (1, right)):
                halves[side, pl.ds(pl.multiple_of(q * GROUP * 4 + v * 8, 8), 8), :] = rows
                inside = jnp.abs(rows[7:8, :] - table[side, 0]) < table[side, 1]
                where = pl.ds(pl.multiple_of((q * (GROUP // 2) + v) * LANES, LANES), LANES)
                onehot[side, :, where] = jnp.where(inside, 1.0, 0.0).astype(BF16)
                weighted = rows * rows[6:7, :]
                terms = jnp.concatenate([weighted[i : i + 1, :] * rows for i in range(PARAMS)], axis=0)
                parts = jnp.concatenate([*split_bf16(terms), jnp.zeros((8, LANES), F32)], axis=0)
                stats[side, :, pl.ds(pl.multiple_of(v * LANES, LANES), LANES)] = parts.astype(BF16)
            return carry

        for v in range(GROUP // 2):
            pair(v, 0)
        for side in range(CORES):
            where = pl.ds(pl.multiple_of(q * (GROUP // 2) * LANES, LANES), (GROUP // 2) * LANES)
            total[side] += lax.dot_general(
                stats[side], onehot[side, :, where], (((1,), (1,)), ((), ())), preferred_element_type=F32
            )

    def arrive(q, carry):
        wait_rows(send_buf, recv_buf, GROUP * 8, send_sem, recv_sem.at[q], partner).wait_recv()
        gather_group(q)
        return carry

    lax.fori_loop(0, groups - 1, arrive, 0)
    wait_rows(send_buf, recv_buf, (GROUP - 1) * 8, send_sem, recv_sem.at[groups - 1], partner).wait_recv()
    gather_group(groups - 1)

    span = PARAMS * 8
    for side in range(CORES):
        sums[side * span : (side + 1) * span, :] = (
            total[side, 0:span, :] + total[side, span : 2 * span, :] + total[side, 2 * span : 3 * span, :]
        )
    sums_copy = pltpu.make_async_remote_copy(
        src_ref=sums,
        dst_ref=other_sums,
        send_sem=pair_send.at[1],
        recv_sem=pair_recv.at[1],
        device_id=partner,
        device_id_type=MESH,
    )
    sums_copy.start()
    sums_copy.wait_recv()

    def summed(row):
        rows = pl.ds(row, CORES, stride=span)
        return sums[rows, :] + other_sums[rows, :]

    normal = [[None] * PARAMS for _ in range(PARAMS)]
    for i in range(PARAMS):
        for j in range(i, PARAMS):
            entry = summed(i * 8 + j)
            if i == j:
                entry = entry + facts[pl.ds(i, CORES, stride=8), :]
            normal[i][j] = entry
            normal[j][i] = entry
    moments = [summed(i * 8 + PARAMS) for i in range(PARAMS)]
    updates = solve_blocks(normal, moments)
    for i in range(PARAMS):
        update_rows[pl.ds(i, CORES, stride=8), :] = updates[i]
    update_rows[pl.ds(PARAMS, CORES, stride=8), :] = jnp.full((CORES, LANES), -1.0, F32)
    for row in (PARAMS + 1, PARAMS + 2):
        update_rows[pl.ds(row, CORES, stride=8), :] = jnp.zeros((CORES, LANES), F32)
    updates_ref[...] = update_rows[pl.ds(pl.multiple_of(core * 8, 8), 8), :][0:PARAMS, :]

    spread = []
    for side in range(CORES):
        parts = split_bf16(update_rows[side * 8 : side * 8 + 8, :])
        spread.append(jnp.concatenate([*parts, jnp.zeros((8, LANES), F32)], axis=0).astype(BF16))

    square_total[...] = jnp.zeros_like(square_total)

    def refit_group(q):
        fitted = []
        for side in range(CORES):
            where = pl.ds(pl.multiple_of(q * (GROUP // 2) * LANES, LANES), (GROUP // 2) * LANES)
            got = lax.dot_general(
                spread[side], onehot[side, :, where], (((1,), (0,)), ((), ())), preferred_element_type=F32
            )
            fitted.append(got[0:8, :] + got[8:16, :] + got[16:24, :])
        squares = square_total[...]
        for v in range(GROUP // 2):
            fresh = []
            for side in range(CORES):
                rows = halves[side, pl.ds(pl.multiple_of(q * GROUP * 4 + v * 8, 8), 8), :]
                term = rows * fitted[side][:, v * LANES : (v + 1) * LANES]
                line = -jnp.sum(term, axis=0, keepdims=True)
                squares = squares + rows[6:7, :] * line * line
                fresh.append(line)
            left, right = fresh
            at = q * GROUP + v * 2
            fresh_out[at] = jnp.where(low[0:1], left, pltpu.roll(right, LANES // 2, 1))
            fresh_out[at + 1] = jnp.where(low[0:1], pltpu.roll(left, LANES // 2, 1), right)
        square_total[...] = squares

    def fresh_copy(p):
        device, _ = behind(p)
        return pltpu.make_async_remote_copy(
            src_ref=fresh_out.at[p],
            dst_ref=fresh_in.at[me_chip],
            send_sem=back_send.at[0],
            recv_sem=back_recv.at[0],
            device_id=device,
            device_id_type=MESH,
        )

    def square_copy(p):
        device, _ = behind(p)
        return pltpu.make_async_remote_copy(
            src_ref=square_out.at[0],
            dst_ref=square_in.at[me_chip],
            send_sem=back_send.at[1],
            recv_sem=back_recv.at[1],
            device_id=device,
            device_id_type=MESH,
        )

    def send_fresh(p, carry):
        fresh_copy(p).start()
        return carry

    def send_square(p, carry):
        square_copy(p).start()
        return carry

    def leave(q, carry):
        refit_group(q)
        lax.fori_loop(q * GROUP, q * GROUP + GROUP, send_fresh, 0)
        return carry

    lax.fori_loop(0, groups - 1, leave, 0)
    refit_group(groups - 1)
    lax.fori_loop((groups - 1) * GROUP, chips - 1, send_fresh, 0)

    squares = square_total[...]
    count_row = counts_ref[...].astype(F32)
    squares = squares + pltpu.roll(squares, LANES // 2, 1)
    count_row = count_row + pltpu.roll(count_row, LANES // 2, 1)
    square_row = jnp.where(low[0:1], squares, count_row)
    square_out[0] = square_row
    lax.fori_loop(0, chips - 1, send_square, 0)
    square_in[me_chip] = square_row
    fresh_in[me_chip] = fresh_out[chips - 1]

    wait_rows(square_in, square_in, chips - 1, back_send.at[1], back_recv.at[1], partner).wait_recv()
    square_total[...] = jnp.sum(square_in[...], axis=0)
    last_copy = pltpu.make_async_remote_copy(
        src_ref=square_total,
        dst_ref=square_out.at[1],
        send_sem=pair_send.at[2],
        recv_sem=pair_recv.at[2],
        device_id=partner,
        device_id_type=MESH,
    )
    last_copy.start()
    wait_rows(fresh_in, fresh_in, chips - 1, back_send.at[0], back_recv.at[0], partner).wait_recv()
    last_copy.wait_recv()
    whole = square_total[...] + square_out[1]
    square_sum = jnp.sum(jnp.where(low[0:1], whole, 0.0), axis=1, keepdims=True)
    count_sum = jnp.sum(jnp.where(low[0:1], 0.0, whole), axis=1, keepdims=True)
    norm = jnp.sqrt(square_sum / count_sum + 1e-6)
    norm_ref[...] = jnp.broadcast_to(norm, (1, LANES))
    standard_ref[...] = jnp.reshape(fresh_in[...], (chips, LANES)) * jnp.sqrt(weight_ref[...]) / norm

    wait_rows(send_buf, recv_buf, (chips - 1) * 8, send_sem, send_sem, partner).wait_send()
    sums_copy.wait_send()
    last_copy.wait_send()
    wait_rows(fresh_in, fresh_in, chips - 1, back_send.at[0], back_recv.at[0], partner).wait_send()
    wait_rows(square_in, square_in, chips - 1, back_send.at[1], back_recv.at[1], partner).wait_send()


def body(shape, source_id, slot, owner, counts, partials, residual, weight, prior):
    size_x, size_y, size_z = shape
    chips = size_x * size_y * size_z
    groups = chips // GROUP
    square = (chips, LANES)
    vmem = pl.BlockSpec(memory_space=pltpu.VMEM)
    updates, standard, norm = pl.pallas_call(
        functools.partial(kernel, shape),
        out_shape=(
            jax.ShapeDtypeStruct((PARAMS, LANES), F32),
            jax.ShapeDtypeStruct(square, F32),
            jax.ShapeDtypeStruct((1, LANES), F32),
        ),
        in_specs=[vmem] * 8,
        out_specs=(vmem, vmem, vmem),
        scratch_shapes=[
            pltpu.VMEM((chips * 8, LANES), F32),
            pltpu.VMEM((chips * 8, LANES), F32),
            pltpu.VMEM((CORES, chips * 4, LANES), F32),
            pltpu.VMEM((CORES, LANES, chips * LANES // 2), BF16),
            pltpu.VMEM((CORES, LANES, GROUP // 2 * LANES), BF16),
            pltpu.VMEM((CORES, LANES, LANES), F32),
            pltpu.VMEM((CORES, 2, LANES, LANES), F32),
            pltpu.VMEM((CORES * 8, LANES), F32),
            pltpu.VMEM((CORES * PARAMS * 8, LANES), F32),
            pltpu.VMEM((CORES * PARAMS * 8, LANES), F32),
            pltpu.VMEM((CORES * 8, LANES), F32),
            pltpu.VMEM((chips, 1, LANES), F32),
            pltpu.VMEM((chips, 1, LANES), F32),
            pltpu.VMEM((2, 1, LANES), F32),
            pltpu.VMEM((chips, 1, LANES), F32),
            pltpu.VMEM((1, LANES), F32),
            pltpu.SemaphoreType.DMA,
            pltpu.SemaphoreType.DMA((groups,)),
            pltpu.SemaphoreType.DMA((3,)),
            pltpu.SemaphoreType.DMA((3,)),
            pltpu.SemaphoreType.DMA((2,)),
            pltpu.SemaphoreType.DMA((2,)),
        ],
        compiler_params=pltpu.CompilerParams(collective_id=0, has_side_effects=True),
    )(
        source_id.reshape(square),
        slot.reshape(square),
        owner.reshape(-1, LANES),
        counts.reshape(1, LANES),
        partials,
        residual.reshape(square),
        weight.reshape(square),
        prior,
    )
    return updates, standard.reshape(-1), norm[0, 0]


def solution(mesh):
    shape = (mesh.shape["grp"], ROWS_Y, mesh.shape["dev"] // (ROWS_Y * CORES))
    rows = P(("grp", "dev"))
    columns = P(None, ("grp", "dev"))
    in_specs = (rows, rows, P(), rows, columns, rows, rows, columns)
    out_specs = (columns, rows, P())
    return jax.shard_map(
        functools.partial(body, shape), mesh=mesh, in_specs=in_specs, out_specs=out_specs, check_vma=False
    )
```

time: 241 us -> 59.1 us (0.25)
  local copies, waits for them, and re-layouts: 101 us -> 2.74 us
  Pallas kernels: 0 us -> 54.4 us
  waiting for transfers between devices: 39.7 us -> 0 us
  blocking collectives: 35.9 us -> 0 us
  starting transfers between devices: 28.1 us -> 0 us
  matrix products: 21.7 us -> 0 us
  other arithmetic: 9.7 us -> 0 us
    gather x1 -> x0, local copies, waits for them, and re-layouts: 90.5 us -> none  [body(): position = owner[source_id]]
    pallas_call x0 -> x1, Pallas kernels: none -> 54.4 us  [body(): pl.pallas_call(functools.partial(kernel, shape), out_shape=(jax.ShapeDtyp...]
    all_to_all x3 -> x0, waiting for transfers between devices: 39.7 us -> none  [one_exchange(): parts = lax.all_to_all(parts, axis, split_axis=0, concat_axis=0, tiled=True)]
    psum x4 -> x0, blocking collectives: 35.9 us -> none  [by_axis(): value = lax.psum(value, axis)]
    all_to_all x3 -> x0, starting transfers between devices: 28.1 us -> none  [one_exchange(): parts = lax.all_to_all(parts, axis, split_axis=0, concat_axis=0, tiled=True)]
    dot_general x16 -> x0, matrix products: 21.7 us -> none  [the longest x12 17.7 us: spread_rows(): lax.dot_general(table, onehot, (((1,), (1,)), ((), ())), precision=lax.Pr...]
    another operation x10 -> x0, local copies, waits for them, and re-layouts: 3.31 us -> none  [the longest x4 1.99 us: accumulate(): stats = jnp.stack(terms)]
  transfers between devices with their start and end apart: 3 -> 0, of which waited for: 3 -> 0; matrix products, arithmetic and copies ran while one was open for 2% -> 0% of each run, Pallas kernels for 0% -> 0%
where the time goes in v1:
time: 59.1 us; the launch traced here: 58.9 us
  Pallas kernels  54.4 us (92%)
  local copies, waits for them, and re-layouts  2.74 us (5%)
  between operations  1.82 us (3%)
    pallas_call x1, Pallas kernels, body(): pl.pallas_call(functools.partial(kernel, shape), out_shape=(jax.ShapeDtyp...  54.4 us
    unnamed x6, local copies, waits for them, and re-layouts  2.74 us

profile of v1, /device:TPU:1, one launch (start us, length us, event | category | flops | bytes accessed | tf_op | source)
XLA Modules:
  0.0 58.9 jit_solution(4190424692320172587)
XLA Ops:
  0.6 54.4 %shard_map.103 = (f32[5,128]{1,0:T(8,128)}, f32[128,128]{1,0:T(8,128)}, f32[1,128]{1,0:T(1,128)}) custom-call(s32[128,128]{1,0:T(8,128)} %bitcast.10, s32[128,128]{1,0:T(8,128)} %bitcast.11, s32[256,128]{1,0:T(8,128)} %bitcast.9, s32[1,128]{1,0:T(1,128)} %bitcast.15, f32[5,16384]{1,0:T(8,128)} %partials_ref.1, f32[128,128]{1,0:T(8,128)} %bitcast.12, ...), custom_call_target="tpu_custom_call" | custom-call | tf_op jit(solution)/shard_map/pallas_call | solution.py:401
  55.0 0.0 copy-start
  55.0 0.7 %copy-done = f32[5,128]{1,0:T(8,128)S(1)} copy-done((f32[5,128]{1,0:T(8,128)S(1)}, f32[5,128]{1,0:T(8,128)}, u32[]{:S(2)}) %copy-start) | copy-done | bytes 2584
  55.7 0.6 %copy.14 = f32[5,128]{1,0:T(8,128)} copy(f32[5,128]{1,0:T(8,128)S(1)} %copy-done) | data formatting | bytes 5120
  56.3 0.0 copy-start.1
  56.3 1.5 %copy.15 = f32[16384]{0:T(1024)} copy(f32[16384]{0:T(1024)} %bitcast.14) | data formatting | bytes 131072
  57.8 0.0 copy-done.1
Async XLA Ops:
  55.0 0.7 %copy-start = (f32[5,128]{1,0:T(8,128)S(1)}, f32[5,128]{1,0:T(8,128)}, u32[]{:S(2)}) copy-start(f32[5,128]{1,0:T(8,128)} %get-tuple-element.12) | copy-start | bytes 7684
  56.3 1.5 %copy-start.1 = (f32[1,128]{1,0:T(1,128)S(1)}, f32[1,128]{1,0:T(1,128)}, u32[]{:S(2)}) copy-start(f32[1,128]{1,0:T(1,128)} %get-tuple-element.8) | copy-start | bytes 1540

commit v2 on v1

--- a/solution.py
+++ b/solution.py
@@ -14,6 +14,7 @@
 ROWS_Y = 4
 CORES = 2
 PARAMS = 5
+FIELDS = 7
 GROUP = 16
 
 
@@ -61,40 +62,13 @@
 
 def kernel(
     shape,
-    source_ref,
-    slot_ref,
-    owner_ref,
-    counts_ref,
-    partials_ref,
-    residual_ref,
-    weight_ref,
-    prior_ref,
-    updates_ref,
-    standard_ref,
-    norm_ref,
-    send_buf,
-    recv_buf,
-    halves,
-    onehot,
-    stats,
-    total,
-    table,
-    facts,
-    sums,
-    other_sums,
-    update_rows,
-    fresh_out,
-    fresh_in,
-    square_out,
-    square_in,
-    square_total,
-    send_sem,
-    recv_sem,
-    pair_send,
-    pair_recv,
-    back_send,
-    back_recv,
+    *refs,
 ):
+    inputs, (updates_ref, standard_ref, norm_ref) = refs[0:8], refs[8:11]
+    loaded = refs[11:19]
+    (send_buf, recv_buf, halves, onehot, stats, total, table, facts, sums, other_sums) = refs[19:29]
+    (update_rows, fresh_out, fresh_in, square_out, square_in, square_total) = refs[29:35]
+    (load_sem, send_sem, recv_sem, pair_send, pair_recv, back_send, back_recv) = refs[35:42]
     size_x, size_y, size_z = shape
     chips = size_x * size_y * size_z
     groups = chips // GROUP
@@ -105,65 +79,67 @@
     me_z = me_dev // (CORES * size_y)
     me_chip = (me_x * size_z + me_z) * size_y + me_y
 
-    def offset(p):
-        q = p // GROUP
-        inside = GROUP - 1 - p % GROUP
-        dz = (size_z // 2 + ((q + 1) // 2) * (1 - 2 * (q % 2))) % size_z
-        return inside // size_y, inside % size_y, dz
-
-    def place(x, y, z):
-        return (x, (z * size_y + y) * CORES + core), (x * size_z + z) * size_y + y
-
-    def ahead(p):
-        dx, dy, dz = offset(p)
-        return place((me_x + dx) % size_x, (me_y + dy) % size_y, (me_z + dz) % size_z)
-
-    def behind(p):
-        dx, dy, dz = offset(p)
-        return place(
-            (me_x + size_x - dx) % size_x,
-            (me_y + size_y - dy) % size_y,
-            (me_z + size_z - dz) % size_z,
-        )
+    xs = [(me_x + dx) % size_x for dx in range(size_x)]
+    ys = [(me_y + dy) % size_y for dy in range(size_y)]
+
+    def group_z(q):
+        return (size_z // 2 + ((q + 1) // 2) * (1 - 2 * (q % 2))) % size_z
+
+    def in_group(q, count, forward, action):
+        dz = group_z(q)
+        z = (me_z + dz) % size_z if forward else (me_z + size_z - dz) % size_z
+        for slot in range(count):
+            inside = GROUP - 1 - slot
+            dx, dy = inside // size_y, inside % size_y
+            if not forward:
+                dx, dy = (size_x - dx) % size_x, (size_y - dy) % size_y
+            x, y = xs[dx], ys[dy]
+            action(q, slot, (x, (z * size_y + y) * CORES + core), (x * size_z + z) * size_y + y)
+
+    def everywhere(forward, action):
+        def one(q, carry):
+            in_group(q, GROUP, forward, action)
+            return carry
+
+        lax.fori_loop(0, groups - 1, one, 0)
+        in_group(groups - 1, GROUP - 1, forward, action)
 
     partner = (me_x, me_dev + 1 - 2 * core)
     barrier = pltpu.get_barrier_semaphore()
 
-    def greet(p, carry):
-        device, _ = ahead(p)
-        pl.semaphore_signal(barrier, inc=1, device_id=device, device_id_type=MESH)
-        return carry
+    for block in range(chips // 8):
+        recv_buf[pl.ds(block * 64 + FIELDS, 8, stride=8), :] = jnp.zeros((8, LANES), F32)
 
     pl.semaphore_signal(barrier, inc=1, device_id=partner, device_id_type=MESH)
-    lax.fori_loop(0, chips - 1, greet, 0)
+    everywhere(
+        True,
+        lambda q, slot, device, chip: pl.semaphore_signal(barrier, inc=1, device_id=device, device_id_type=MESH),
+    )
+
+    loads = [
+        pltpu.make_async_copy(source, target, load_sem.at[index])
+        for index, (source, target) in enumerate(zip(inputs, loaded, strict=True))
+    ]
+    for load in loads:
+        load.start()
+    source_ref, slot_ref, owner_ref, counts_ref, partials_ref, residual_ref, weight_ref, prior_ref = loaded
+    for load in loads:
+        load.wait()
 
     for block in range(chips // 8):
         rows = pl.ds(block * 8, 8)
+        root = jnp.sqrt(weight_ref[rows, :])
         cell = (source_ref[rows, :] * LANES + slot_ref[rows, :]).astype(F32)
-        send_buf[pl.ds(block * 64 + PARAMS, 8, stride=8), :] = residual_ref[rows, :]
-        send_buf[pl.ds(block * 64 + PARAMS + 1, 8, stride=8), :] = weight_ref[rows, :]
-        send_buf[pl.ds(block * 64 + PARAMS + 2, 8, stride=8), :] = cell
-        for tile in range(block * 8, block * 8 + 8):
-            send_buf[tile * 8 : tile * 8 + PARAMS, :] = partials_ref[:, tile * LANES : (tile + 1) * LANES]
+        send_buf[pl.ds(block * 64 + PARAMS, 8, stride=8), :] = residual_ref[rows, :] * root
+        send_buf[pl.ds(block * 64 + PARAMS + 1, 8, stride=8), :] = cell
+        for row in range(8):
+            tile = block * 8 + row
+            send_buf[tile * 8 : tile * 8 + PARAMS, :] = (
+                partials_ref[:, tile * LANES : (tile + 1) * LANES] * root[row : row + 1, :]
+            )
     facts[pl.ds(pl.multiple_of(core * 8, 8), 8), :] = jnp.concatenate(
         [prior_ref[...], counts_ref[...].astype(F32), jnp.zeros((2, LANES), F32)], axis=0
     )
-
-    sublane = lax.broadcasted_iota(jnp.int32, (LANES, LANES), 0)
-    lane = lax.broadcasted_iota(jnp.int32, (1, LANES), 1)
-    for side in range(CORES):
-        base = (me_chip * CORES + side) * LANES
-
-        def look(step, found):
-            rows = owner_ref[pl.ds(pl.multiple_of(step * 8, 8), 8), :] - base
-            for row in range(8):
-                here = lane + (step * 8 + row) * LANES
-                found = jnp.where(rows[row : row + 1, :] == sublane, here, found)
-            return found
-
-        found = lax.fori_loop(0, owner_ref.shape[0] // 8, look, jnp.zeros((LANES, LANES), jnp.int32))
-        first = jnp.sum(found.astype(F32), axis=1, keepdims=True) * LANES
-        table[side, 0] = jnp.broadcast_to(first, (LANES, LANES))
 
     pl.semaphore_wait(barrier, chips)
 
@@ -177,23 +153,34 @@
     )
     facts_copy.start()
 
-    def tile_copy(p):
-        device, chip = ahead(p)
-        return pltpu.make_async_remote_copy(
-            src_ref=send_buf.at[pl.ds(pl.multiple_of(chip * 8, 8), 8), :],
-            dst_ref=recv_buf.at[pl.ds(pl.multiple_of(p * 8, 8), 8), :],
+    def send_tile(q, slot, device, chip):
+        pltpu.make_async_remote_copy(
+            src_ref=send_buf.at[pl.ds(pl.multiple_of(chip * 8, 8), FIELDS), :],
+            dst_ref=recv_buf.at[pl.ds(pl.multiple_of(q * (GROUP * 8), 8) + slot * 8, FIELDS), :],
             send_sem=send_sem,
-            recv_sem=recv_sem.at[p // GROUP],
+            recv_sem=recv_sem.at[q],
             device_id=device,
             device_id_type=MESH,
-        )
-
-    def send_tile(p, carry):
-        tile_copy(p).start()
-        return carry
-
-    lax.fori_loop(0, chips - 1, send_tile, 0)
-    recv_buf[(chips - 1) * 8 : chips * 8, :] = send_buf[pl.ds(pl.multiple_of(me_chip * 8, 8), 8), :]
+        ).start()
+
+    everywhere(True, send_tile)
+    recv_buf[(chips - 1) * 8 : chips * 8 - 1, :] = send_buf[pl.ds(pl.multiple_of(me_chip * 8, 8), 8), :][0:FIELDS, :]
+
+    sublane = lax.broadcasted_iota(jnp.int32, (LANES, LANES), 0)
+    lane = lax.broadcasted_iota(jnp.int32, (1, LANES), 1)
+    for side in range(CORES):
+        base = (me_chip * CORES + side) * LANES
+
+        def look(step, found):
+            rows = owner_ref[pl.ds(pl.multiple_of(step * 8, 8), 8), :] - base
+            for row in range(8):
+                here = lane + (step * 8 + row) * LANES
+                found = jnp.where(rows[row : row + 1, :] == sublane, here, found)
+            return found
+
+        found = lax.fori_loop(0, owner_ref.shape[0] // 8, look, jnp.zeros((LANES, LANES), jnp.int32))
+        first = jnp.sum(found.astype(F32), axis=1, keepdims=True) * LANES
+        table[side, 0] = jnp.broadcast_to(first, (LANES, LANES))
 
     facts_copy.wait()
     for side in range(CORES):
@@ -223,11 +210,10 @@
             right = jnp.where(low, pltpu.roll(even, LANES // 2, 1), odd)
             for side, rows in ((0, left), (1, right)):
                 halves[side, pl.ds(pl.multiple_of(q * GROUP * 4 + v * 8, 8), 8), :] = rows
-                inside = jnp.abs(rows[7:8, :] - table[side, 0]) < table[side, 1]
+                inside = jnp.abs(rows[6:7, :] - table[side, 0]) < table[side, 1]
                 where = pl.ds(pl.multiple_of((q * (GROUP // 2) + v) * LANES, LANES), LANES)
                 onehot[side, :, where] = jnp.where(inside, 1.0, 0.0).astype(BF16)
-                weighted = rows * rows[6:7, :]
-                terms = jnp.concatenate([weighted[i : i + 1, :] * rows for i in range(PARAMS)], axis=0)
+                terms = jnp.concatenate([rows[i : i + 1, :] * rows for i in range(PARAMS)], axis=0)
                 parts = jnp.concatenate([*split_bf16(terms), jnp.zeros((8, LANES), F32)], axis=0)
                 stats[side, :, pl.ds(pl.multiple_of(v * LANES, LANES), LANES)] = parts.astype(BF16)
             return carry
@@ -241,12 +227,12 @@
             )
 
     def arrive(q, carry):
-        wait_rows(send_buf, recv_buf, GROUP * 8, send_sem, recv_sem.at[q], partner).wait_recv()
+        wait_rows(send_buf, recv_buf, GROUP * FIELDS, send_sem, recv_sem.at[q], partner).wait_recv()
         gather_group(q)
         return carry
 
     lax.fori_loop(0, groups - 1, arrive, 0)
-    wait_rows(send_buf, recv_buf, (GROUP - 1) * 8, send_sem, recv_sem.at[groups - 1], partner).wait_recv()
+    wait_rows(send_buf, recv_buf, (GROUP - 1) * FIELDS, send_sem, recv_sem.at[groups - 1], partner).wait_recv()
     gather_group(groups - 1)
 
     span = PARAMS * 8
@@ -308,7 +294,7 @@
                 rows = halves[side, pl.ds(pl.multiple_of(q * GROUP * 4 + v * 8, 8), 8), :]
                 term = rows * fitted[side][:, v * LANES : (v + 1) * LANES]
                 line = -jnp.sum(term, axis=0, keepdims=True)
-                squares = squares + rows[6:7, :] * line * line
+                squares = squares + line * line
                 fresh.append(line)
             left, right = fresh
             at = q * GROUP + v * 2
@@ -316,78 +302,67 @@
             fresh_out[at + 1] = jnp.where(low[0:1], pltpu.roll(left, LANES // 2, 1), right)
         square_total[...] = squares
 
-    def fresh_copy(p):
-        device, _ = behind(p)
-        return pltpu.make_async_remote_copy(
-            src_ref=fresh_out.at[p],
+    def send_fresh(q, slot, device, chip):
+        pltpu.make_async_remote_copy(
+            src_ref=fresh_out.at[q * GROUP + slot],
             dst_ref=fresh_in.at[me_chip],
             send_sem=back_send.at[0],
             recv_sem=back_recv.at[0],
             device_id=device,
             device_id_type=MESH,
-        )
-
-    def square_copy(p):
-        device, _ = behind(p)
-        return pltpu.make_async_remote_copy(
-            src_ref=square_out.at[0],
+        ).start()
+
+    def send_square(q, slot, device, chip):
+        pltpu.make_async_remote_copy(
+            src_ref=square_out.at[2],
             dst_ref=square_in.at[me_chip],
             send_sem=back_send.at[1],
             recv_sem=back_recv.at[1],
             device_id=device,
             device_id_type=MESH,
-        )
-
-    def send_fresh(p, carry):
-        fresh_copy(p).start()
-        return carry
-
-    def send_square(p, carry):
-        square_copy(p).start()
-        return carry
+        ).start()
 
     def leave(q, carry):
         refit_group(q)
-        lax.fori_loop(q * GROUP, q * GROUP + GROUP, send_fresh, 0)
+        in_group(q, GROUP, False, send_fresh)
         return carry
 
     lax.fori_loop(0, groups - 1, leave, 0)
     refit_group(groups - 1)
-    lax.fori_loop((groups - 1) * GROUP, chips - 1, send_fresh, 0)
 
     squares = square_total[...]
     count_row = counts_ref[...].astype(F32)
     squares = squares + pltpu.roll(squares, LANES // 2, 1)
     count_row = count_row + pltpu.roll(count_row, LANES // 2, 1)
-    square_row = jnp.where(low[0:1], squares, count_row)
-    square_out[0] = square_row
-    lax.fori_loop(0, chips - 1, send_square, 0)
-    square_in[me_chip] = square_row
-    fresh_in[me_chip] = fresh_out[chips - 1]
-
-    wait_rows(square_in, square_in, chips - 1, back_send.at[1], back_recv.at[1], partner).wait_recv()
-    square_total[...] = jnp.sum(square_in[...], axis=0)
-    last_copy = pltpu.make_async_remote_copy(
-        src_ref=square_total,
+    square_out[0] = jnp.where(low[0:1], squares, count_row)
+    square_copy = pltpu.make_async_remote_copy(
+        src_ref=square_out.at[0],
         dst_ref=square_out.at[1],
         send_sem=pair_send.at[2],
         recv_sem=pair_recv.at[2],
         device_id=partner,
         device_id_type=MESH,
     )
-    last_copy.start()
+    square_copy.start()
+    in_group(groups - 1, GROUP - 1, False, send_fresh)
+    square_copy.wait_recv()
+    square_row = square_out[0] + square_out[1]
+    square_out[2] = square_row
+    everywhere(False, send_square)
+    square_in[me_chip] = square_row
+    fresh_in[me_chip] = fresh_out[chips - 1]
     wait_rows(fresh_in, fresh_in, chips - 1, back_send.at[0], back_recv.at[0], partner).wait_recv()
-    last_copy.wait_recv()
-    whole = square_total[...] + square_out[1]
+    wait_rows(square_in, square_in, chips - 1, back_send.at[1], back_recv.at[1], partner).wait_recv()
+    whole = jnp.sum(square_in[...], axis=0)
     square_sum = jnp.sum(jnp.where(low[0:1], whole, 0.0), axis=1, keepdims=True)
     count_sum = jnp.sum(jnp.where(low[0:1], 0.0, whole), axis=1, keepdims=True)
     norm = jnp.sqrt(square_sum / count_sum + 1e-6)
     norm_ref[...] = jnp.broadcast_to(norm, (1, LANES))
-    standard_ref[...] = jnp.reshape(fresh_in[...], (chips, LANES)) * jnp.sqrt(weight_ref[...]) / norm
-
-    wait_rows(send_buf, recv_buf, (chips - 1) * 8, send_sem, send_sem, partner).wait_send()
+    standard_ref[...] = jnp.reshape(fresh_in[...], (chips, LANES)) / norm
+
+    wait_rows(send_buf, recv_buf, (chips - 1) * FIELDS, send_sem, send_sem, partner).wait_send()
     sums_copy.wait_send()
-    last_copy.wait_send()
+    square_copy.wait_send()
     wait_rows(fresh_in, fresh_in, chips - 1, back_send.at[0], back_recv.at[0], partner).wait_send()
     wait_rows(square_in, square_in, chips - 1, back_send.at[1], back_recv.at[1], partner).wait_send()
 
@@ -397,6 +372,16 @@
     chips = size_x * size_y * size_z
     groups = chips // GROUP
     square = (chips, LANES)
+    arrays = (
+        source_id.reshape(square),
+        slot.reshape(square),
+        owner.reshape(-1, LANES),
+        counts.reshape(1, LANES),
+        partials,
+        residual.reshape(square),
+        weight.reshape(square),
+        prior,
+    )
     vmem = pl.BlockSpec(memory_space=pltpu.VMEM)
     updates, standard, norm = pl.pallas_call(
         functools.partial(kernel, shape),
@@ -405,9 +390,10 @@
             jax.ShapeDtypeStruct(square, F32),
             jax.ShapeDtypeStruct((1, LANES), F32),
         ),
-        in_specs=[vmem] * 8,
+        in_specs=[pl.BlockSpec(memory_space=pl.ANY)] * 8,
         out_specs=(vmem, vmem, vmem),
-        scratch_shapes=[
+        scratch_shapes=[pltpu.VMEM(array.shape, array.dtype) for array in arrays]
+        + [
             pltpu.VMEM((chips * 8, LANES), F32),
             pltpu.VMEM((chips * 8, LANES), F32),
             pltpu.VMEM((CORES, chips * 4, LANES), F32),
@@ -421,9 +407,10 @@
             pltpu.VMEM((CORES * 8, LANES), F32),
             pltpu.VMEM((chips, 1, LANES), F32),
             pltpu.VMEM((chips, 1, LANES), F32),
-            pltpu.VMEM((2, 1, LANES), F32),
+            pltpu.VMEM((3, 1, LANES), F32),
             pltpu.VMEM((chips, 1, LANES), F32),
             pltpu.VMEM((1, LANES), F32),
+            pltpu.SemaphoreType.DMA((8,)),
             pltpu.SemaphoreType.DMA,
             pltpu.SemaphoreType.DMA((groups,)),
             pltpu.SemaphoreType.DMA((3,)),
@@ -432,16 +419,7 @@
             pltpu.SemaphoreType.DMA((2,)),
         ],
         compiler_params=pltpu.CompilerParams(collective_id=0, has_side_effects=True),
-    )(
-        source_id.reshape(square),
-        slot.reshape(square),
-        owner.reshape(-1, LANES),
-        counts.reshape(1, LANES),
-        partials,
-        residual.reshape(square),
-        weight.reshape(square),
-        prior,
-    )
+    )(*arrays)
     return updates, standard.reshape(-1), norm[0, 0]
 
 

time: 59.1 us -> 46.5 us (0.79)
  Pallas kernels: 54.4 us -> 41.7 us
    pallas_call x1, Pallas kernels: 54.4 us -> 41.7 us  [body(): pl.pallas_call(functools.partial(kernel, shape), out_shape=(jax.ShapeDtyp...]
where the time goes in v2:
time: 46.5 us; the launch traced here: 46.3 us
  Pallas kernels  41.7 us (90%)
  local copies, waits for them, and re-layouts  2.74 us (6%)
  between operations  1.82 us (4%)
    pallas_call x1, Pallas kernels, body(): pl.pallas_call(functools.partial(kernel, shape), out_shape=(jax.ShapeDtyp...  41.7 us
    unnamed x6, local copies, waits for them, and re-layouts  2.74 us

profile of v2, /device:TPU:1, one launch (start us, length us, event | category | flops | bytes accessed | tf_op | source)
XLA Modules:
  0.0 46.3 jit_solution(10125806225697205148)
XLA Ops:
  0.6 41.7 %shard_map.103 = (f32[5,128]{1,0:T(8,128)}, f32[128,128]{1,0:T(8,128)}, f32[1,128]{1,0:T(1,128)}) custom-call(s32[128,128]{1,0:T(8,128)} %bitcast.10, s32[128,128]{1,0:T(8,128)} %bitcast.11, s32[256,128]{1,0:T(8,128)} %bitcast.9, s32[1,128]{1,0:T(1,128)} %bitcast.15, f32[5,16384]{1,0:T(8,128)} %refs_4_.1, f32[128,128]{1,0:T(8,128)} %bitcast.12, ...), custom_call_target="tpu_custom_call" | custom-call | tf_op jit(solution)/shard_map/pallas_call | solution.py:386
  42.4 0.0 copy-start
  42.4 0.7 %copy-done = f32[5,128]{1,0:T(8,128)S(1)} copy-done((f32[5,128]{1,0:T(8,128)S(1)}, f32[5,128]{1,0:T(8,128)}, u32[]{:S(2)}) %copy-start) | copy-done | bytes 2584
  43.1 0.6 %copy.14 = f32[5,128]{1,0:T(8,128)} copy(f32[5,128]{1,0:T(8,128)S(1)} %copy-done) | data formatting | bytes 5120
  43.6 0.0 copy-start.1
  43.6 1.5 %copy.15 = f32[16384]{0:T(1024)} copy(f32[16384]{0:T(1024)} %bitcast.14) | data formatting | bytes 131072
  45.1 0.0 copy-done.1
Async XLA Ops:
  42.4 0.7 %copy-start = (f32[5,128]{1,0:T(8,128)S(1)}, f32[5,128]{1,0:T(8,128)}, u32[]{:S(2)}) copy-start(f32[5,128]{1,0:T(8,128)} %get-tuple-element.12) | copy-start | bytes 7684
  43.6 1.5 %copy-start.1 = (f32[1,128]{1,0:T(1,128)S(1)}, f32[1,128]{1,0:T(1,128)}, u32[]{:S(2)}) copy-start(f32[1,128]{1,0:T(1,128)} %get-tuple-element.8) | copy-start | bytes 1540

commit v3 on v2

v3 whole, which is shorter than its diff:
```python
import functools

import jax
import jax.numpy as jnp
from jax import lax
from jax.experimental import pallas as pl
from jax.experimental.pallas import tpu as pltpu
from jax.sharding import PartitionSpec as P

MESH = pl.DeviceIdType.MESH
F32 = jnp.float32
BF16 = jnp.bfloat16
LANES = 128
ROWS_Y = 4
CORES = 2
PARAMS = 5
FIELDS = 7
GROUP = 16
WIDE = GROUP // 2 * LANES
PACK = 16


def split_bf16(value):
    high = value.astype(BF16).astype(F32)
    rest = value - high
    middle = rest.astype(BF16).astype(F32)
    return high, middle, rest - middle


def column_of(row):
    square = (LANES, LANES)
    diagonal = lax.broadcasted_iota(jnp.int32, square, 0) == lax.broadcasted_iota(jnp.int32, square, 1)
    return jnp.sum(jnp.where(diagonal, jnp.broadcast_to(row, square), 0.0), axis=1, keepdims=True)


def solve_blocks(normal, moments):
    params = len(moments)
    factor = {}
    for column in range(params):
        running = normal[column][column]
        for earlier in range(column):
            running = running - factor[column, earlier] ** 2
        pivot_value = jnp.sqrt(running)
        factor[column, column] = pivot_value
        for target in range(column + 1, params):
            current = normal[target][column]
            for earlier in range(column):
                current = current - factor[target, earlier] * factor[column, earlier]
            factor[target, column] = current / pivot_value
    forward = []
    for target in range(params):
        current = moments[target]
        for earlier in range(target):
            current = current - factor[target, earlier] * forward[earlier]
        forward.append(current / factor[target, target])
    backward = [None] * params
    for target in reversed(range(params)):
        current = forward[target]
        for later in range(target + 1, params):
            current = current - factor[later, target] * backward[later]
        backward[target] = current / factor[target, target]
    return backward


def send_order(shape):
    size_x, size_y, size_z = shape
    far_x, far_y, far_z = (
        sorted(range(size), key=lambda step: (-min(step, size - step), step)) for size in (size_x, size_y, size_z)
    )
    return [(dx, dy, dz) for dy in far_y for dz in far_z for dx in far_x]


def kernel(
    shape,
    *refs,
):
    inputs, (updates_ref, standard_ref, norm_ref) = refs[0:8], refs[8:11]
    loaded = refs[11:19]
    (send_buf, recv_buf, halves, onehot, stats, total, table, facts, sums, other_sums) = refs[19:29]
    (update_rows, fresh_out, fresh_in, squares_mine, squares_other) = refs[29:34]
    (load_sem, send_sem, recv_sem, pair_send, pair_recv, back_send, back_recv) = refs[34:41]
    size_x, size_y, size_z = shape
    chips = size_x * size_y * size_z
    groups = chips // GROUP
    me_x = lax.axis_index("grp")
    me_dev = lax.axis_index("dev")
    core = me_dev % CORES
    me_y = (me_dev // CORES) % size_y
    me_z = me_dev // (CORES * size_y)
    me_chip = (me_x * size_z + me_z) * size_y + me_y


    xs = [(me_x + dx) % size_x for dx in range(size_x)]
    ys = [(me_y + dy) % size_y for dy in range(size_y)]
    zs = [(me_z + dz) % size_z for dz in range(size_z)]
    offsets = send_order(shape)

    def everywhere(forward, action):
        for slot, (dx, dy, dz) in enumerate(offsets[:-1]):
            if not forward:
                dx, dy, dz = (size_x - dx) % size_x, (size_y - dy) % size_y, (size_z - dz) % size_z
            action(slot, xs[dx], zs[dz] * size_y + ys[dy])

    partner = (me_x, me_dev + 1 - 2 * core)
    barrier = pltpu.get_barrier_semaphore()

    loads = [
        pltpu.make_async_copy(source, target, load_sem.at[index])
        for index, (source, target) in enumerate(zip(inputs, loaded, strict=True))
    ]
    for load in loads:
        load.start()
    for block in range(chips // 8):
        recv_buf[pl.ds(block * 64 + FIELDS, 8, stride=8), :] = jnp.zeros((8, LANES), F32)

    pl.semaphore_signal(barrier, inc=1, device_id=partner, device_id_type=MESH)
    everywhere(
        True,
        lambda slot, x, zy: pl.semaphore_signal(
            barrier, inc=1, device_id=(x, zy * CORES + core), device_id_type=MESH
        ),
    )

    source_ref, slot_ref, owner_ref, counts_ref, partials_ref, residual_ref, weight_ref, prior_ref = loaded
    for load in loads:
        load.wait()

    for block in range(chips // 8):
        rows = pl.ds(block * 8, 8)
        root = jnp.sqrt(weight_ref[rows, :])
        cell = (source_ref[rows, :] * LANES + slot_ref[rows, :]).astype(F32)
        send_buf[pl.ds(block * 64 + PARAMS, 8, stride=8), :] = residual_ref[rows, :] * root
        send_buf[pl.ds(block * 64 + PARAMS + 1, 8, stride=8), :] = cell
        for row in range(8):
            tile = block * 8 + row
            send_buf[tile * 8 : tile * 8 + PARAMS, :] = (
                partials_ref[:, tile * LANES : (tile + 1) * LANES] * root[row : row + 1, :]
            )
    facts[pl.ds(pl.multiple_of(core * 8, 8), 8), :] = jnp.concatenate(
        [prior_ref[...], counts_ref[...].astype(F32), jnp.zeros((2, LANES), F32)], axis=0
    )

    pl.semaphore_wait(barrier, chips)

    facts_copy = pltpu.make_async_remote_copy(
        src_ref=facts.at[pl.ds(pl.multiple_of(core * 8, 8), 8), :],
        dst_ref=facts.at[pl.ds(pl.multiple_of(core * 8, 8), 8), :],
        send_sem=pair_send.at[0],
        recv_sem=pair_recv.at[0],
        device_id=partner,
        device_id_type=MESH,
    )
    facts_copy.start()

    def send_tile(slot, x, zy):
        chip = x * (size_z * size_y) + zy
        pltpu.make_async_remote_copy(
            src_ref=send_buf.at[pl.ds(pl.multiple_of(chip * 8, 8), FIELDS), :],
            dst_ref=recv_buf.at[pl.ds(slot * 8, FIELDS), :],
            send_sem=send_sem,
            recv_sem=recv_sem.at[slot // GROUP],
            device_id=(x, zy * CORES + core),
            device_id_type=MESH,
        ).start()

    everywhere(True, send_tile)
    recv_buf[(chips - 1) * 8 : chips * 8 - 1, :] = send_buf[pl.ds(pl.multiple_of(me_chip * 8, 8), 8), :][0:FIELDS, :]

    sublane = lax.broadcasted_iota(jnp.int32, (LANES, LANES), 0)
    lane = lax.broadcasted_iota(jnp.int32, (1, LANES), 1)
    for side in range(CORES):
        base = (me_chip * CORES + side) * LANES

        def look(step, found):
            rows = owner_ref[pl.ds(pl.multiple_of(step * 8, 8), 8), :] - base
            for row in range(8):
                here = lane + (step * 8 + row) * LANES
                found = jnp.where(rows[row : row + 1, :] == sublane, here, found)
            return found

        found = lax.fori_loop(0, owner_ref.shape[0] // 8, look, jnp.zeros((LANES, LANES), jnp.int32))
        first = jnp.sum(found.astype(F32), axis=1, keepdims=True)
        table[side, 0] = jnp.broadcast_to(first, (LANES, LANES)).astype(jnp.int32).astype(jnp.int16)

    facts_copy.wait()
    for side in range(CORES):
        count = column_of(facts[side * 8 + PARAMS : side * 8 + PARAMS + 1, :])
        table[side, 1] = jnp.broadcast_to(count, (LANES, LANES)).astype(jnp.int32).astype(jnp.int16)

    def wait_rows(source, target, count, send, recv, to):
        return pltpu.make_async_remote_copy(
            src_ref=source.at[pl.ds(0, count)],
            dst_ref=target.at[pl.ds(0, count)],
            send_sem=send,
            recv_sem=recv,
            device_id=to,
            device_id_type=MESH,
        )

    low = lax.broadcasted_iota(jnp.int32, (8, LANES), 1) < LANES // 2
    total[...] = jnp.zeros_like(total)

    def gather_group(q):
        sides = ([], [])
        for v in range(GROUP // 2):
            start = (q * GROUP + v * 2) * 8
            even = recv_buf[start : start + 8, :]
            odd = recv_buf[start + 8 : start + 16, :]
            sides[0].append(jnp.where(low, even, pltpu.roll(odd, LANES // 2, 1)))
            sides[1].append(jnp.where(low, pltpu.roll(even, LANES // 2, 1), odd))
        for side in range(CORES):
            sources, slots = [], []
            for v, rows in enumerate(sides[side]):
                place = (q * (GROUP // 2) + v) * 8
                halves[side, place : place + 8, :] = rows
                cell = jnp.broadcast_to(rows[FIELDS - 1 : FIELDS, :], (PACK, LANES)).astype(jnp.int32)
                sources.append((cell // LANES).astype(jnp.int16))
                slots.append((cell % LANES).astype(jnp.int16))
                terms = jnp.concatenate([rows[i : i + 1, :] * rows for i in range(PARAMS)], axis=0)
                parts = jnp.concatenate([*split_bf16(terms), jnp.zeros((8, LANES), F32)], axis=0)
                stats[side, :, q * WIDE + v * LANES : q * WIDE + (v + 1) * LANES] = parts.astype(BF16)
            for part in range(LANES // PACK):
                picked = slice(part * PACK, (part + 1) * PACK)
                source, count = table[side, 0, picked, :], table[side, 1, picked, :]
                for v in range(GROUP // 2):
                    inside = (sources[v] == source) & (slots[v] < count)
                    onehot[side, picked, q * WIDE + v * LANES : q * WIDE + (v + 1) * LANES] = jnp.where(
                        inside, jnp.ones((PACK, LANES), BF16), jnp.zeros((PACK, LANES), BF16)
                    )

    def sum_group(q):
        for side in range(CORES):
            where = slice(q * WIDE, (q + 1) * WIDE)
            total[side] += lax.dot_general(
                stats[side, :, where],
                onehot[side, :, where],
                (((1,), (1,)), ((), ())),
                preferred_element_type=F32,
            )

    order = list(range(groups))
    for at, q in enumerate(order):
        count = GROUP - 1 if q == groups - 1 else GROUP
        wait_rows(send_buf, recv_buf, count * FIELDS, send_sem, recv_sem.at[q], partner).wait_recv()
        gather_group(q)
        if at > 0:
            sum_group(order[at - 1])
    sum_group(order[-1])

    span = PARAMS * 8
    for side in range(CORES):
        sums[side * span : (side + 1) * span, :] = (
            total[side, 0:span, :] + total[side, span : 2 * span, :] + total[side, 2 * span : 3 * span, :]
        )
    sums_copy = pltpu.make_async_remote_copy(
        src_ref=sums,
        dst_ref=other_sums,
        send_sem=pair_send.at[1],
        recv_sem=pair_recv.at[1],
        device_id=partner,
        device_id_type=MESH,
    )
    sums_copy.start()
    sums_copy.wait_recv()

    def summed(row):
        rows = pl.ds(row, CORES, stride=span)
        return sums[rows, :] + other_sums[rows, :]

    normal = [[None] * PARAMS for _ in range(PARAMS)]
    for i in range(PARAMS):
        for j in range(i, PARAMS):
            entry = summed(i * 8 + j)
            if i == j:
                entry = entry + facts[pl.ds(i, CORES, stride=8), :]
            normal[i][j] = entry
            normal[j][i] = entry
    moments = [summed(i * 8 + PARAMS) for i in range(PARAMS)]
    updates = solve_blocks(normal, moments)
    for i in range(PARAMS):
        update_rows[pl.ds(i, CORES, stride=8), :] = updates[i]
    update_rows[pl.ds(PARAMS, CORES, stride=8), :] = jnp.full((CORES, LANES), -1.0, F32)
    for row in (PARAMS + 1, PARAMS + 2):
        update_rows[pl.ds(row, CORES, stride=8), :] = jnp.zeros((CORES, LANES), F32)
    updates_ref[...] = update_rows[pl.ds(pl.multiple_of(core * 8, 8), 8), :][0:PARAMS, :]

    spread = []
    for side in range(CORES):
        parts = split_bf16(update_rows[side * 8 : side * 8 + 8, :])
        spread.append(jnp.concatenate([*parts, jnp.zeros((8, LANES), F32)], axis=0).astype(BF16))

    squares = jnp.zeros((1, LANES), F32)
    for q in range(groups):
        fitted = []
        for side in range(CORES):
            got = lax.dot_general(
                spread[side],
                onehot[side, :, q * WIDE : (q + 1) * WIDE],
                (((1,), (0,)), ((), ())),
                preferred_element_type=F32,
            )
            fitted.append(got[0:8, :] + got[8:16, :] + got[16:24, :])
        for v in range(GROUP // 2):
            fresh = []
            for side in range(CORES):
                rows = halves[side, (q * GROUP // 2 + v) * 8 : (q * GROUP // 2 + v + 1) * 8, :]
                term = rows * fitted[side][:, v * LANES : (v + 1) * LANES]
                line = -jnp.sum(term, axis=0, keepdims=True)
                squares = squares + line * line
                fresh.append(line)
            left, right = fresh
            at = q * GROUP + v * 2
            fresh_out[at, 0:1] = jnp.where(low[0:1], left, pltpu.roll(right, LANES // 2, 1))
            fresh_out[at + 1, 0:1] = jnp.where(low[0:1], pltpu.roll(left, LANES // 2, 1), right)
    count_row = counts_ref[...].astype(F32)
    squares = squares + pltpu.roll(squares, LANES // 2, 1)
    count_row = count_row + pltpu.roll(count_row, LANES // 2, 1)
    square_row = jnp.where(low[0:1], squares, count_row)
    for slot in range(chips):
        fresh_out[slot, 1:2] = square_row

    def send_fresh(slot, x, zy):
        pltpu.make_async_remote_copy(
            src_ref=fresh_out.at[slot],
            dst_ref=fresh_in.at[me_chip],
            send_sem=back_send,
            recv_sem=back_recv,
            device_id=(x, zy * CORES + core),
            device_id_type=MESH,
        ).start()

    everywhere(False, send_fresh)
    fresh_in[me_chip] = fresh_out[chips - 1]
    wait_rows(fresh_in, fresh_in, chips - 1, back_send, back_recv, partner).wait_recv()
    squares_mine[...] = jnp.sum(fresh_in[:, 1, :], axis=0, keepdims=True)
    square_copy = pltpu.make_async_remote_copy(
        src_ref=squares_mine,
        dst_ref=squares_other,
        send_sem=pair_send.at[2],
        recv_sem=pair_recv.at[2],
        device_id=partner,
        device_id_type=MESH,
    )
    square_copy.start()
    fresh = fresh_in[:, 0, :]
    square_copy.wait_recv()
    whole = squares_mine[...] + squares_other[...]
    square_sum = jnp.sum(jnp.where(low[0:1], whole, 0.0), axis=1, keepdims=True)
    count_sum = jnp.sum(jnp.where(low[0:1], 0.0, whole), axis=1, keepdims=True)
    norm = jnp.sqrt(square_sum / count_sum + 1e-6)
    norm_ref[...] = jnp.broadcast_to(norm, (1, LANES))
    standard_ref[...] = fresh / norm

    wait_rows(send_buf, recv_buf, (chips - 1) * FIELDS, send_sem, send_sem, partner).wait_send()
    sums_copy.wait_send()
    square_copy.wait_send()
    wait_rows(fresh_in, fresh_in, chips - 1, back_send, back_recv, partner).wait_send()


def finish(*refs):
    copies = [
        pltpu.make_async_copy(source, target, refs[6].at[index])
        for index, (source, target) in enumerate(zip(refs[0:3], refs[3:6], strict=True))
    ]
    for copy in copies:
        copy.start()
    for copy in copies:
        copy.wait()


def body(shape, source_id, slot, owner, counts, partials, residual, weight, prior):
    size_x, size_y, size_z = shape
    chips = size_x * size_y * size_z
    groups = chips // GROUP
    square = (chips, LANES)
    arrays = (
        source_id.reshape(square),
        slot.reshape(square),
        owner.reshape(-1, LANES),
        counts.reshape(1, LANES),
        partials,
        residual.reshape(square),
        weight.reshape(square),
        prior,
    )
    vmem = pl.BlockSpec(memory_space=pltpu.VMEM)
    results = (
        jax.ShapeDtypeStruct((PARAMS, LANES), F32),
        jax.ShapeDtypeStruct(square, F32),
        jax.ShapeDtypeStruct((1, LANES), F32),
    )
    exchanged = pl.pallas_call(
        functools.partial(kernel, shape),
        out_shape=tuple(pltpu.VMEM(result.shape, result.dtype) for result in results),
        in_specs=[pl.BlockSpec(memory_space=pl.ANY)] * 8,
        out_specs=(vmem, vmem, vmem),
        scratch_shapes=[pltpu.VMEM(array.shape, array.dtype) for array in arrays]
        + [
            pltpu.VMEM((chips * 8, LANES), F32),
            pltpu.VMEM((chips * 8, LANES), F32),
            pltpu.VMEM((CORES, chips * 4, LANES), F32),
            pltpu.VMEM((CORES, LANES, chips * LANES // 2), BF16),
            pltpu.VMEM((CORES, LANES, chips * LANES // 2), BF16),
            pltpu.VMEM((CORES, LANES, LANES), F32),
            pltpu.VMEM((CORES, 2, LANES, LANES), jnp.int16),
            pltpu.VMEM((CORES * 8, LANES), F32),
            pltpu.VMEM((CORES * PARAMS * 8, LANES), F32),
            pltpu.VMEM((CORES * PARAMS * 8, LANES), F32),
            pltpu.VMEM((CORES * 8, LANES), F32),
            pltpu.VMEM((chips, 2, LANES), F32),
            pltpu.VMEM((chips, 2, LANES), F32),
            pltpu.VMEM((1, LANES), F32),
            pltpu.VMEM((1, LANES), F32),
            pltpu.SemaphoreType.DMA((8,)),
            pltpu.SemaphoreType.DMA,
            pltpu.SemaphoreType.DMA((groups,)),
            pltpu.SemaphoreType.DMA((3,)),
            pltpu.SemaphoreType.DMA((3,)),
            pltpu.SemaphoreType.DMA,
            pltpu.SemaphoreType.DMA,
        ],
        compiler_params=pltpu.CompilerParams(collective_id=0, has_side_effects=True),
    )(*arrays)
    place = pl.BlockSpec(memory_space=pl.ANY)
    updates, standard, norm = pl.pallas_call(
        finish,
        out_shape=results,
        in_specs=[place] * 3,
        out_specs=(place, place, place),
        scratch_shapes=[pltpu.SemaphoreType.DMA((3,))],
    )(*(pltpu.with_memory_space_constraint(value, pltpu.VMEM) for value in exchanged))
    return updates, standard.reshape(-1), norm[0, 0]


def solution(mesh):
    shape = (mesh.shape["grp"], ROWS_Y, mesh.shape["dev"] // (ROWS_Y * CORES))
    rows = P(("grp", "dev"))
    columns = P(None, ("grp", "dev"))
    in_specs = (rows, rows, P(), rows, columns, rows, rows, columns)
    out_specs = (columns, rows, P())
    return jax.shard_map(
        functools.partial(body, shape), mesh=mesh, in_specs=in_specs, out_specs=out_specs, check_vma=False
    )
```

time: 46.5 us -> 39.9 us (0.86)
  local copies, waits for them, and re-layouts: 2.74 us -> 0 us
  Pallas kernels: 41.7 us -> 39.2 us
  between operations: 1.82 us -> 0.64 us
    unnamed x6 -> x0, local copies, waits for them, and re-layouts: 2.74 us -> none
    pallas_call x1 -> x2, Pallas kernels: 41.7 us -> 39.2 us  [the longest x1 38.5 us: body(): pl.pallas_call(functools.partial(kernel, shape), out_shape=tuple((pltpu.V...]
where the time goes in v3:
time: 39.9 us; the launch traced here: 39.8 us
  Pallas kernels  39.2 us (98%)
  between operations  0.64 us (2%)
    pallas_call x1, Pallas kernels, body(): pl.pallas_call(functools.partial(kernel, shape), out_shape=tuple((pltpu.V...  38.5 us

profile of v3, /device:TPU:1, one launch (start us, length us, event | category | flops | bytes accessed | tf_op | source)
XLA Modules:
  0.0 39.8 jit_solution(15157889639477248475)
XLA Ops:
  0.6 38.5 %shard_map.103 = (f32[5,128]{1,0:T(8,128)S(1)}, f32[128,128]{1,0:T(8,128)S(1)}, f32[1,128]{1,0:T(1,128)S(1)}) custom-call(s32[128,128]{1,0:T(8,128)} %bitcast.10, s32[128,128]{1,0:T(8,128)} %bitcast.11, s32[256,128]{1,0:T(8,128)} %bitcast.9, s32[1,128]{1,0:T(1,128)} %bitcast.14, f32[5,16384]{1,0:T(8,128)} %refs_4_.1, f32[128,128]{1,0:T(8,128)} %bitcast.12, ...), custom_call_target="tpu_custom_call" | custom-call | tf_op jit(solution)/shard_map/pallas_call | solution.py:392
  39.2 0.7 %shard_map.104 = (f32[5,128]{1,0:T(8,128)}, f32[128,128]{1,0:T(8,128)}, f32[1,128]{1,0:T(1,128)}) custom-call(f32[5,128]{1,0:T(8,128)S(1)} %get-tuple-element.9.refs_0_, f32[128,128]{1,0:T(8,128)S(1)} %get-tuple-element.10.refs_1_, f32[1,128]{1,0:T(1,128)S(1)} %get-tuple-element.11.refs_2_), custom_call_target="tpu_custom_call" | custom-call | tf_op jit(solution)/shard_map/pallas_call | solution.py:425

commit v4 on v3

--- a/solution.py
+++ b/solution.py
@@ -62,12 +62,18 @@
     return backward
 
 
+def hops(offset, shape):
+    return sum(min(step, size - step) for step, size in zip(offset, shape, strict=True))
+
+
 def send_order(shape):
     size_x, size_y, size_z = shape
-    far_x, far_y, far_z = (
-        sorted(range(size), key=lambda step: (-min(step, size - step), step)) for size in (size_x, size_y, size_z)
-    )
-    return [(dx, dy, dz) for dy in far_y for dz in far_z for dx in far_x]
+    reach = size_z // 4
+    every = [(x, y, z) for y in range(size_y) for z in range(size_z) for x in range(size_x)]
+    every.sort(key=lambda offset: -hops(offset, shape))
+    near = [offset for offset in every[:-1] if min(offset[2], size_z - offset[2]) <= reach]
+    far = [offset for offset in every[:-1] if offset not in near]
+    return near, far, [(0, 0, reach), (0, 0, size_z - reach)]
 
 
 def kernel(
@@ -78,7 +84,7 @@
     loaded = refs[11:19]
     (send_buf, recv_buf, halves, onehot, stats, total, table, facts, sums, other_sums) = refs[19:29]
     (update_rows, fresh_out, fresh_in, squares_mine, squares_other) = refs[29:34]
-    (load_sem, send_sem, recv_sem, pair_send, pair_recv, back_send, back_recv) = refs[34:41]
+    (load_sem, send_sem, recv_sem, pair_send, pair_recv, back_send, back_recv, vouched) = refs[34:42]
     size_x, size_y, size_z = shape
     chips = size_x * size_y * size_z
     groups = chips // GROUP
@@ -93,13 +99,17 @@
     xs = [(me_x + dx) % size_x for dx in range(size_x)]
     ys = [(me_y + dy) % size_y for dy in range(size_y)]
     zs = [(me_z + dz) % size_z for dz in range(size_z)]
-    offsets = send_order(shape)
-
-    def everywhere(forward, action):
-        for slot, (dx, dy, dz) in enumerate(offsets[:-1]):
-            if not forward:
-                dx, dy, dz = (size_x - dx) % size_x, (size_y - dy) % size_y, (size_z - dz) % size_z
-            action(slot, xs[dx], zs[dz] * size_y + ys[dy])
+    near, far, vouchers = send_order(shape)
+    offsets = near + far
+    nearby, beyond = range(len(near)), range(len(near), len(offsets))
+
+    def ahead(offset):
+        dx, dy, dz = offset
+        return xs[dx], zs[dz] * size_y + ys[dy]
+
+    def behind(offset):
+        dx, dy, dz = offset
+        return ahead(((size_x - dx) % size_x, (size_y - dy) % size_y, (size_z - dz) % size_z))
 
     partner = (me_x, me_dev + 1 - 2 * core)
     barrier = pltpu.get_barrier_semaphore()
@@ -114,12 +124,9 @@
         recv_buf[pl.ds(block * 64 + FIELDS, 8, stride=8), :] = jnp.zeros((8, LANES), F32)
 
     pl.semaphore_signal(barrier, inc=1, device_id=partner, device_id_type=MESH)
-    everywhere(
-        True,
-        lambda slot, x, zy: pl.semaphore_signal(
-            barrier, inc=1, device_id=(x, zy * CORES + core), device_id_type=MESH
-        ),
-    )
+    for offset in near:
+        x, zy = ahead(offset)
+        pl.semaphore_signal(barrier, inc=1, device_id=(x, zy * CORES + core), device_id_type=MESH)
 
     source_ref, slot_ref, owner_ref, counts_ref, partials_ref, residual_ref, weight_ref, prior_ref = loaded
     for load in loads:
@@ -140,7 +147,10 @@
         [prior_ref[...], counts_ref[...].astype(F32), jnp.zeros((2, LANES), F32)], axis=0
     )
 
-    pl.semaphore_wait(barrier, chips)
+    pl.semaphore_wait(barrier, len(near) + 1)
+    for offset in vouchers:
+        x, zy = behind(offset)
+        pl.semaphore_signal(vouched, inc=1, device_id=(x, zy * CORES + core), device_id_type=MESH)
 
     facts_copy = pltpu.make_async_remote_copy(
         src_ref=facts.at[pl.ds(pl.multiple_of(core * 8, 8), 8), :],
@@ -152,7 +162,8 @@
     )
     facts_copy.start()
 
-    def send_tile(slot, x, zy):
+    def send_tile(slot):
+        x, zy = ahead(offsets[slot])
         chip = x * (size_z * size_y) + zy
         pltpu.make_async_remote_copy(
             src_ref=send_buf.at[pl.ds(pl.multiple_of(chip * 8, 8), FIELDS), :],
@@ -163,7 +174,11 @@
             device_id_type=MESH,
         ).start()
 
-    everywhere(True, send_tile)
+    for slot in nearby:
+        send_tile(slot)
+    pl.semaphore_wait(vouched, len(vouchers))
+    for slot in beyond:
+        send_tile(slot)
     recv_buf[(chips - 1) * 8 : chips * 8 - 1, :] = send_buf[pl.ds(pl.multiple_of(me_chip * 8, 8), 8), :][0:FIELDS, :]
 
     sublane = lax.broadcasted_iota(jnp.int32, (LANES, LANES), 0)
@@ -319,7 +334,8 @@
     for slot in range(chips):
         fresh_out[slot, 1:2] = square_row
 
-    def send_fresh(slot, x, zy):
+    def send_fresh(slot):
+        x, zy = behind(offsets[slot])
         pltpu.make_async_remote_copy(
             src_ref=fresh_out.at[slot],
             dst_ref=fresh_in.at[me_chip],
@@ -329,7 +345,8 @@
             device_id_type=MESH,
         ).start()
 
-    everywhere(False, send_fresh)
+    for slot in sorted(range(chips - 1), key=lambda slot: -hops(offsets[slot], shape)):
+        send_fresh(slot)
     fresh_in[me_chip] = fresh_out[chips - 1]
     wait_rows(fresh_in, fresh_in, chips - 1, back_send, back_recv, partner).wait_recv()
     squares_mine[...] = jnp.sum(fresh_in[:, 1, :], axis=0, keepdims=True)
@@ -418,6 +435,7 @@
             pltpu.SemaphoreType.DMA((3,)),
             pltpu.SemaphoreType.DMA,
             pltpu.SemaphoreType.DMA,
+            pltpu.SemaphoreType.REGULAR,
         ],
         compiler_params=pltpu.CompilerParams(collective_id=0, has_side_effects=True),
     )(*arrays)

time: 39.9 us -> 39.3 us (0.985)
  Pallas kernels: 39.2 us -> 38.6 us
    pallas_call x1, Pallas kernels: 38.5 us -> 37.9 us  [body(): pl.pallas_call(functools.partial(kernel, shape), out_shape=tuple((pltpu.V...]
where the time goes in v4:
time: 39.3 us; the launch traced here: 39.2 us
  Pallas kernels  38.6 us (98%)
  between operations  0.64 us (2%)
    pallas_call x1, Pallas kernels, body(): pl.pallas_call(functools.partial(kernel, shape), out_shape=tuple((pltpu.V...  37.9 us

profile of v4, /device:TPU:1, one launch (start us, length us, event | category | flops | bytes accessed | tf_op | source)
XLA Modules:
  0.0 39.2 jit_solution(11584293915444813217)
XLA Ops:
  0.6 37.9 %shard_map.103 = (f32[5,128]{1,0:T(8,128)S(1)}, f32[128,128]{1,0:T(8,128)S(1)}, f32[1,128]{1,0:T(1,128)S(1)}) custom-call(s32[128,128]{1,0:T(8,128)} %bitcast.10, s32[128,128]{1,0:T(8,128)} %bitcast.11, s32[256,128]{1,0:T(8,128)} %bitcast.9, s32[1,128]{1,0:T(1,128)} %bitcast.14, f32[5,16384]{1,0:T(8,128)} %refs_4_.1, f32[128,128]{1,0:T(8,128)} %bitcast.12, ...), custom_call_target="tpu_custom_call" | custom-call | tf_op jit(solution)/shard_map/pallas_call | solution.py:409
  38.6 0.7 %shard_map.104 = (f32[5,128]{1,0:T(8,128)}, f32[128,128]{1,0:T(8,128)}, f32[1,128]{1,0:T(1,128)}) custom-call(f32[5,128]{1,0:T(8,128)S(1)} %get-tuple-element.9.refs_0_, f32[128,128]{1,0:T(8,128)S(1)} %get-tuple-element.10.refs_1_, f32[1,128]{1,0:T(1,128)S(1)} %get-tuple-element.11.refs_2_), custom_call_target="tpu_custom_call" | custom-call | tf_op jit(solution)/shard_map/pallas_call | solution.py:443

commit v5 on v4

--- a/solution.py
+++ b/solution.py
@@ -10,6 +10,7 @@
 MESH = pl.DeviceIdType.MESH
 F32 = jnp.float32
 BF16 = jnp.bfloat16
+F8 = jnp.float8_e4m3fn
 LANES = 128
 ROWS_Y = 4
 CORES = 2
@@ -82,9 +83,9 @@
 ):
     inputs, (updates_ref, standard_ref, norm_ref) = refs[0:8], refs[8:11]
     loaded = refs[11:19]
-    (send_buf, recv_buf, halves, onehot, stats, total, table, facts, sums, other_sums) = refs[19:29]
-    (update_rows, fresh_out, fresh_in, squares_mine, squares_other) = refs[29:34]
-    (load_sem, send_sem, recv_sem, pair_send, pair_recv, back_send, back_recv, vouched) = refs[34:42]
+    (send_buf, recv_buf, halves, onehot, total, table, facts, sums, other_sums) = refs[19:28]
+    (update_rows, fresh_out, fresh_in, squares_mine, squares_other) = refs[28:33]
+    (load_sem, send_sem, recv_sem, pair_send, pair_recv, back_send, back_recv, vouched) = refs[33:41]
     size_x, size_y, size_z = shape
     chips = size_x * size_y * size_z
     groups = chips // GROUP
@@ -224,7 +225,7 @@
             sides[0].append(jnp.where(low, even, pltpu.roll(odd, LANES // 2, 1)))
             sides[1].append(jnp.where(low, pltpu.roll(even, LANES // 2, 1), odd))
         for side in range(CORES):
-            sources, slots = [], []
+            sources, slots, terms_of, picked_of = [], [], [], [[] for _ in range(GROUP // 2)]
             for v, rows in enumerate(sides[side]):
                 place = (q * (GROUP // 2) + v) * 8
                 halves[side, place : place + 8, :] = rows
@@ -233,34 +234,27 @@
                 slots.append((cell % LANES).astype(jnp.int16))
                 terms = jnp.concatenate([rows[i : i + 1, :] * rows for i in range(PARAMS)], axis=0)
                 parts = jnp.concatenate([*split_bf16(terms), jnp.zeros((8, LANES), F32)], axis=0)
-                stats[side, :, q * WIDE + v * LANES : q * WIDE + (v + 1) * LANES] = parts.astype(BF16)
+                terms_of.append(parts.astype(BF16))
             for part in range(LANES // PACK):
                 picked = slice(part * PACK, (part + 1) * PACK)
                 source, count = table[side, 0, picked, :], table[side, 1, picked, :]
                 for v in range(GROUP // 2):
                     inside = (sources[v] == source) & (slots[v] < count)
-                    onehot[side, picked, q * WIDE + v * LANES : q * WIDE + (v + 1) * LANES] = jnp.where(
-                        inside, jnp.ones((PACK, LANES), BF16), jnp.zeros((PACK, LANES), BF16)
-                    )
-
-    def sum_group(q):
-        for side in range(CORES):
-            where = slice(q * WIDE, (q + 1) * WIDE)
+                    mark = jnp.where(inside, jnp.ones((PACK, LANES), BF16), jnp.zeros((PACK, LANES), BF16))
+                    onehot[side, picked, q * WIDE + v * LANES : q * WIDE + (v + 1) * LANES] = mark.astype(F8)
+                    picked_of[v].append(mark)
             total[side] += lax.dot_general(
-                stats[side, :, where],
-                onehot[side, :, where],
+                jnp.concatenate(terms_of, axis=1),
+                jnp.concatenate([jnp.concatenate(marks, axis=0) for marks in picked_of], axis=1),
                 (((1,), (1,)), ((), ())),
                 preferred_element_type=F32,
             )
 
     order = list(range(groups))
-    for at, q in enumerate(order):
+    for q in order:
         count = GROUP - 1 if q == groups - 1 else GROUP
         wait_rows(send_buf, recv_buf, count * FIELDS, send_sem, recv_sem.at[q], partner).wait_recv()
         gather_group(q)
-        if at > 0:
-            sum_group(order[at - 1])
-    sum_group(order[-1])
 
     span = PARAMS * 8
     for side in range(CORES):
@@ -416,8 +410,7 @@
             pltpu.VMEM((chips * 8, LANES), F32),
             pltpu.VMEM((chips * 8, LANES), F32),
             pltpu.VMEM((CORES, chips * 4, LANES), F32),
-            pltpu.VMEM((CORES, LANES, chips * LANES // 2), BF16),
-            pltpu.VMEM((CORES, LANES, chips * LANES // 2), BF16),
+            pltpu.VMEM((CORES, LANES, chips * LANES // 2), F8),
             pltpu.VMEM((CORES, LANES, LANES), F32),
             pltpu.VMEM((CORES, 2, LANES, LANES), jnp.int16),
             pltpu.VMEM((CORES * 8, LANES), F32),

time: 39.3 us -> 38.8 us (0.987)
  Pallas kernels: 38.6 us -> 38.1 us
    pallas_call x1, Pallas kernels: 37.9 us -> 37.4 us  [body(): pl.pallas_call(functools.partial(kernel, shape), out_shape=tuple((pltpu.V...]
where the time goes in v5:
time: 38.8 us; the launch traced here: 38.7 us
  Pallas kernels  38.1 us (98%)
  between operations  0.64 us (2%)
    pallas_call x1, Pallas kernels, body(): pl.pallas_call(functools.partial(kernel, shape), out_shape=tuple((pltpu.V...  37.4 us

profile of v5, /device:TPU:1, one launch (start us, length us, event | category | flops | bytes accessed | tf_op | source)
XLA Modules:
  0.0 38.7 jit_solution(1123357583858456698)
XLA Ops:
  0.6 37.4 %shard_map.103 = (f32[5,128]{1,0:T(8,128)S(1)}, f32[128,128]{1,0:T(8,128)S(1)}, f32[1,128]{1,0:T(1,128)S(1)}) custom-call(s32[128,128]{1,0:T(8,128)} %bitcast.10, s32[128,128]{1,0:T(8,128)} %bitcast.11, s32[256,128]{1,0:T(8,128)} %bitcast.9, s32[1,128]{1,0:T(1,128)} %bitcast.14, f32[5,16384]{1,0:T(8,128)} %refs_4_.1, f32[128,128]{1,0:T(8,128)} %bitcast.12, ...), custom_call_target="tpu_custom_call" | custom-call | tf_op jit(solution)/shard_map/pallas_call | solution.py:403
  38.1 0.7 %shard_map.104 = (f32[5,128]{1,0:T(8,128)}, f32[128,128]{1,0:T(8,128)}, f32[1,128]{1,0:T(1,128)}) custom-call(f32[5,128]{1,0:T(8,128)S(1)} %get-tuple-element.9.refs_0_, f32[128,128]{1,0:T(8,128)S(1)} %get-tuple-element.10.refs_1_, f32[1,128]{1,0:T(1,128)S(1)} %get-tuple-element.11.refs_2_), custom_call_target="tpu_custom_call" | custom-call | tf_op jit(solution)/shard_map/pallas_call | solution.py:436

commit v6 on v5

--- a/solution.py
+++ b/solution.py
@@ -101,8 +101,9 @@
     ys = [(me_y + dy) % size_y for dy in range(size_y)]
     zs = [(me_z + dz) % size_z for dz in range(size_z)]
     near, far, vouchers = send_order(shape)
-    offsets = near + far
-    nearby, beyond = range(len(near)), range(len(near), len(offsets))
+    own = len(near)
+    offsets = near + [(0, 0, 0)] + far
+    nearby, beyond = range(own), range(own + 1, chips)
 
     def ahead(offset):
         dx, dy, dz = offset
@@ -180,7 +181,7 @@
     pl.semaphore_wait(vouched, len(vouchers))
     for slot in beyond:
         send_tile(slot)
-    recv_buf[(chips - 1) * 8 : chips * 8 - 1, :] = send_buf[pl.ds(pl.multiple_of(me_chip * 8, 8), 8), :][0:FIELDS, :]
+    recv_buf[own * 8 : own * 8 + FIELDS, :] = send_buf[pl.ds(pl.multiple_of(me_chip * 8, 8), 8), :][0:FIELDS, :]
 
     sublane = lax.broadcasted_iota(jnp.int32, (LANES, LANES), 0)
     lane = lax.broadcasted_iota(jnp.int32, (1, LANES), 1)
@@ -252,7 +253,7 @@
 
     order = list(range(groups))
     for q in order:
-        count = GROUP - 1 if q == groups - 1 else GROUP
+        count = GROUP - 1 if q == own // GROUP else GROUP
         wait_rows(send_buf, recv_buf, count * FIELDS, send_sem, recv_sem.at[q], partner).wait_recv()
         gather_group(q)
 
@@ -339,9 +340,9 @@
             device_id_type=MESH,
         ).start()
 
-    for slot in sorted(range(chips - 1), key=lambda slot: -hops(offsets[slot], shape)):
+    for slot in sorted([*nearby, *beyond], key=lambda slot: -hops(offsets[slot], shape)):
         send_fresh(slot)
-    fresh_in[me_chip] = fresh_out[chips - 1]
+    fresh_in[me_chip] = fresh_out[own]
     wait_rows(fresh_in, fresh_in, chips - 1, back_send, back_recv, partner).wait_recv()
     squares_mine[...] = jnp.sum(fresh_in[:, 1, :], axis=0, keepdims=True)
     square_copy = pltpu.make_async_remote_copy(

time: 38.8 us -> 38.9 us (level)
  no operation moved by 1% of the time
where the time goes in v6:
time: 38.9 us; the launch traced here: 38.8 us
  Pallas kernels  38.1 us (98%)
  between operations  0.64 us (2%)
    pallas_call x1, Pallas kernels, body(): pl.pallas_call(functools.partial(kernel, shape), out_shape=tuple((pltpu.V...  37.5 us

profile of v6, /device:TPU:1, one launch (start us, length us, event | category | flops | bytes accessed | tf_op | source)
XLA Modules:
  0.0 38.8 jit_solution(13492325229427987285)
XLA Ops:
  0.6 37.5 %shard_map.103 = (f32[5,128]{1,0:T(8,128)S(1)}, f32[128,128]{1,0:T(8,128)S(1)}, f32[1,128]{1,0:T(1,128)S(1)}) custom-call(s32[128,128]{1,0:T(8,128)} %bitcast.10, s32[128,128]{1,0:T(8,128)} %bitcast.11, s32[256,128]{1,0:T(8,128)} %bitcast.9, s32[1,128]{1,0:T(1,128)} %bitcast.14, f32[5,16384]{1,0:T(8,128)} %refs_4_.1, f32[128,128]{1,0:T(8,128)} %bitcast.12, ...), custom_call_target="tpu_custom_call" | custom-call | tf_op jit(solution)/shard_map/pallas_call | solution.py:404
  38.1 0.7 %shard_map.104 = (f32[5,128]{1,0:T(8,128)}, f32[128,128]{1,0:T(8,128)}, f32[1,128]{1,0:T(1,128)}) custom-call(f32[5,128]{1,0:T(8,128)S(1)} %get-tuple-element.9.refs_0_, f32[128,128]{1,0:T(8,128)S(1)} %get-tuple-element.10.refs_1_, f32[1,128]{1,0:T(1,128)S(1)} %get-tuple-element.11.refs_2_), custom_call_target="tpu_custom_call" | custom-call | tf_op jit(solution)/shard_map/pallas_call | solution.py:437
